TPU v7x, 32 devices: a whole 2x2x4 slice. The times are simulated.
32 devices in a mesh: dp: 2 (over x), ctx: 4 (over y, core), tp: 4 (over z).
Axes of the slice: x: 2, y: 2, z: 4, core: 2. Of those that a mesh axis runs over, the one named last changes fastest.
Arguments:
- layer_input: bfloat16 [2, 1024, 8192], P('dp', ('ctx', 'tp')), may hold values from -6 to 6
- value_weight: bfloat16 [8192, 1024], P(('dp', 'ctx'), 'tp'), may hold values from -0.0625 to 0.0625
- query_raw: bfloat16 [2, 1024, 1024], P('dp', 'ctx', 'tp'), may hold values from -6 to 6
- key_raw: bfloat16 [2, 1024, 1024], P('dp', 'ctx', 'tp'), may hold values from -6 to 6
- out_grad: bfloat16 [2, 1024, 1024], P('dp', 'ctx', 'tp'), may hold values from -6 to 6
- gate_logits: float32 [2, 2, 8, 1024], P(None, 'dp', 'tp', 'ctx'), may hold values from -14 to 4, as said below
- decay_params: float32 [2, 8], P(None, 'tp'), may hold values from -0.35 to 0.35
- saved_states: float32 [2, 4, 8, 128, 128], P('dp', 'ctx', 'tp'), may hold values from -4 to 4
Outputs:
- input_grad: bfloat16 [2, 1024, 8192], P('dp', ('ctx', 'tp'))
- query_grad: bfloat16 [2, 1024, 1024], P('dp', 'ctx', 'tp')
- key_grad: bfloat16 [2, 1024, 1024], P('dp', 'ctx', 'tp')
- gate_grad: float32 [2, 2, 8, 1024], P(None, 'dp', 'tp', 'ctx')
- decay_grad: float32 [2, 8], P(None, 'tp')
Inputs may be any that keep to these rules, and one draw needn't show every extreme that they name: `gate_logits`: row 0 holds decay logits, row 1 write-strength logits.
All inputs are finite; a program needn't handle non-finite values.
Results may differ from a plain program's by a relative error of at most 0.015.
Values may be sent and summed in bfloat16 or wider, within the bound.
No kernel may reach another device: no remote copies, remote signals or barrier semaphores. Data moves between devices by JAX's collectives and lax.ppermute only.
A program may use at most 64 MiB of HBM per device.

v0:
```python
import functools
import jax
import jax.numpy as jnp
from jax import lax
from jax.experimental import pallas as pl
from jax.experimental.pallas import tpu as pltpu
from jax.sharding import PartitionSpec as P


f32 = jnp.float32
bf16 = jnp.bfloat16
epsilon = 1e-06
BASE = 8
LOW = 64


def place_core():
    return lax.axis_index("ctx") & 1


def place_chip():
    return lax.axis_index("dp") * (lax.axis_size("ctx") // 2) + (lax.axis_index("ctx") >> 1)


def place_level():
    return lax.axis_index("tp")


def mm(a, b, ca=1, cb=0):
    return lax.dot_general(
        a.astype(bf16), b.astype(bf16), (((ca,), (cb,)), ((), ())), preferred_element_type=f32
    )


def halves(a):
    high = a.astype(bf16)
    return high, (a - high.astype(f32)).astype(bf16)


def mm3(a, b, ca=1, cb=0):
    ah, al = halves(a)
    bh, bl = halves(b)
    return mm(ah, bh, ca, cb) + (mm(ah, bl, ca, cb) + mm(al, bh, ca, cb))


def softplus(x):
    return jnp.maximum(x, 0.0) + jnp.log(1.0 + jnp.exp(-jnp.abs(x)))


def sigmoid(x):
    return 1.0 / (1.0 + jnp.exp(-x))


def positions(n):
    return (
        lax.broadcasted_iota(jnp.int32, (n, n), 0),
        lax.broadcasted_iota(jnp.int32, (n, n), 1),
    )


def stack_rows(rows):
    n = rows[0].shape[1]
    short = -len(rows) % 8
    return jnp.concatenate(list(rows) + [jnp.zeros((1, n), f32)] * short, axis=0)


def to_columns(rows):
    turned = stack_rows(rows).T
    return [turned[:, i : i + 1] for i in range(len(rows))]


def to_rows(columns):
    n = columns[0].shape[0]
    short = -len(columns) % 8
    turned = jnp.concatenate(list(columns) + [jnp.zeros((n, 1), f32)] * short, axis=1).T
    return [turned[i : i + 1] for i in range(len(columns))]


def gate_rows(gates_ref, params_ref, heads):
    out = []
    for h in range(heads):
        ga = gates_ref[0, h : h + 1, :]
        gb = gates_ref[1, h : h + 1, :]
        scale = jnp.exp(jnp.broadcast_to(params_ref[0:1, h : h + 1], ga.shape))
        shifted = ga + params_ref[1:2, h : h + 1]
        out.append((-scale * softplus(shifted), sigmoid(gb), -scale * sigmoid(shifted)))
    return out


def cumulated(logs, i, j):
    return [jnp.sum(jnp.where(j <= i, row, 0.0), axis=1, keepdims=True) for row in logs]


def thirds(ref):
    n = ref.shape[0] // 3
    return [ref.at[index * n : (index + 1) * n] for index in range(3)]


def units(ref, h, hd):
    raw = ref[:, h * hd : (h + 1) * hd].astype(f32)
    inv = lax.rsqrt(jnp.sum(raw * raw, axis=-1, keepdims=True) + epsilon)
    return raw, inv


def folded(a, i, j, size):
    a = jnp.where((i ^ j) < size, a, 0.0)
    return functools.reduce(jnp.add, [a[g : g + size] for g in range(0, a.shape[0], size)])


def dot_blocks(a, b, keep):
    def spread(part):
        return jnp.concatenate([part] * (part.shape[1] // part.shape[0]), axis=0) * keep

    ah, al = halves(a)
    bh, bl = [spread(part) for part in halves(b)]
    return mm(ah, bh) + (mm(ah, bl) + mm(al, bh))


def inverse_upper(strict, i, j):
    n = strict[0].shape[0]
    size = min(LOW, n)

    def frame(size):
        r = lax.broadcasted_iota(jnp.int32, (size, n), 0)
        c = lax.broadcasted_iota(jnp.int32, (size, n), 1) & (size - 1)
        keep = ((i ^ j) < size).astype(f32).astype(bf16)
        return r ^ c, keep, [folded(a, i, j, size) for a in strict]

    apart, keep, parts = frame(size)
    power = [jnp.where(apart < BASE, a, 0.0) for a in parts]
    result = [(apart == 0).astype(f32) - a for a in power]
    k = 2
    while k < BASE:
        power = [dot_blocks(a, a, keep) for a in power]
        result = [u + dot_blocks(u, a, keep) for u, a in zip(result, power)]
        k *= 2
    b = BASE
    while 2 * b < n:
        if 2 * b > size:
            size = 2 * b
            apart, keep, parts = frame(size)
            result = [
                jnp.where(apart < b, jnp.concatenate([u, u], axis=0), 0.0) for u in result
            ]
        cross = (apart < 2 * b) & (apart >= b)
        part = [dot_blocks(u, jnp.where(cross, a, 0.0), keep) for u, a in zip(result, parts)]
        result = [u - dot_blocks(x, u, keep) for u, x in zip(result, part)]
        b *= 2
    out = []
    part = [mm3(u[:, :b], a[:b, b:]) for u, a in zip(result, strict)]
    part = [mm3(x, u[:, b:]) for u, x in zip(result, part)]
    for u, x in zip(result, part):
        top = jnp.concatenate([u[:, :b], -x], axis=1)
        low = jnp.concatenate([jnp.zeros((b, b), f32), u[:, b:]], axis=1)
        out.append(jnp.concatenate([top, low], axis=0))
    return out


def shared(gates_ref, params_ref, heads, i, j):
    rows = gate_rows(gates_ref, params_ref, heads)
    sums = cumulated([r[0] for r in rows], i, j)
    sum_rows = to_rows(sums)
    strength_cols = to_columns([r[1] for r in rows])
    return rows, sums, sum_rows, strength_cols


def kernel_a(gates_ref, params_ref, tokens_ref, bc_ref, x_ref, z_ref, u_ref):
    q_ref, k_ref, g_ref = thirds(tokens_ref)
    heads, hd = bc_ref.shape[0], bc_ref.shape[1]
    n = q_ref.shape[0]
    i, j = positions(n)
    rows, sums, sum_rows, strengths = shared(gates_ref, params_ref, heads, i, j)
    strict, scores, ks, qs = [], [], [], []
    for h in range(heads):
        qraw, qinv = units(q_ref, h, hd)
        kraw, kinv = units(k_ref, h, hd)
        q = qraw * qinv * hd ** (-0.5)
        k = kraw * kinv
        fade = jnp.where(i <= j, jnp.exp(jnp.where(i <= j, sum_rows[h] - sums[h], 0.0)), 0.0)
        strict.append(jnp.where(i < j, fade * rows[h][1] * mm(k, k, 1, 1), 0.0))
        scores.append(fade * mm(k, q, 1, 1))
        ks.append(k)
        qs.append(q)
    inverse = inverse_upper(strict, i, j)
    ei, ej = positions(hd)
    for h in range(heads):
        last = sums[h][n - 1 : n, :]
        tail = jnp.exp(last - sums[h])
        grown = jnp.exp(sums[h])
        cot = g_ref[:, h * hd : (h + 1) * hd]
        right = jnp.concatenate([ks[h] * tail, mm(scores[h], cot)], axis=1)
        x = mm(inverse[h], right)
        y = mm(strengths[h] * grown * ks[h], x, 0, 0)
        b = jnp.where(ei == ej, jnp.exp(last), 0.0) - y[:, :hd]
        c = mm(qs[h] * grown, cot, 0, 0) - y[:, hd:]
        bc_ref[h] = jnp.concatenate([b, c], axis=1).astype(bf16)
        x_ref[h] = x[:, :hd].astype(bf16)
        z_ref[h] = x[:, hd:]
        u_ref[h] = inverse[h]


def kernel_compose(bc_ref, other_ref, *outs, full):
    heads, hd = bc_ref.shape[0], bc_ref.shape[1]
    first = jnp.full((hd, 2 * hd), place_core(), jnp.int32) == 0
    for h in range(heads):
        a = bc_ref[h].astype(f32)
        b = other_ref[h].astype(f32)
        early = jnp.where(first, a, b)
        late = jnp.where(first, b, a)
        joined = mm(early[:, :hd], late if full else late[:, hd:])
        c = joined[:, -hd:] + early[:, hd:]
        outs[0][h] = c.astype(bf16)
        if full:
            outs[1][h] = jnp.concatenate([joined[:, :hd], c], axis=1).astype(bf16)


def kernel_b(gates_ref, x_ref, z0_ref, other_ref, *refs, count, steps):
    received = refs[:count]
    outs = refs[count : count + steps]
    z_ref, end_ref, dv_ref = refs[count + steps :]
    heads, n, hd = x_ref.shape
    me = place_level()
    last = jnp.full((hd, hd), place_core(), jnp.int32) == 1
    strengths = to_columns([sigmoid(gates_ref[1, h : h + 1, :]) for h in range(heads)])
    for h in range(heads):
        end = jnp.zeros((hd, hd), f32)
        for index, ref in reversed(list(enumerate(received))):
            if index == count - 1:
                end = ref[h].astype(f32)
            else:
                end = mm(ref[h, :, :hd], end) + ref[h, :, hd:].astype(f32)
        inner = mm(other_ref[h, :, :hd], end) + other_ref[h, :, hd:].astype(f32)
        end = jnp.where(last, end, inner)
        z = z0_ref[h] + mm(x_ref[h], end)
        z_ref[h] = z
        end_ref[h] = end
        dv_ref[:, h * hd : (h + 1) * hd] = strengths[h] * z
    block = n // steps
    for m in range(steps):
        at = pl.multiple_of((me ^ m) * block, block)
        outs[m][...] = dv_ref[pl.ds(at, block), :].astype(bf16)


def kernel_pre(
    gates_ref,
    params_ref,
    tokens_ref,
    s_ref,
    u_ref,
    z_ref,
    end_ref,
    ut_ref,
    fade_ref,
    sink_ref,
    gram_ref,
    cross_ref,
    ks_ref,
    qn_ref,
    kn_ref,
    dq_ref,
    dk_ref,
    kend_ref,
    side_ref,
):
    q_ref, k_ref, g_ref = thirds(tokens_ref)
    heads, n, hd = z_ref.shape
    i, j = positions(n)
    rows, sums, sum_rows, strengths = shared(gates_ref, params_ref, heads, i, j)
    sides = []
    for h in range(heads):
        qraw, qinv = units(q_ref, h, hd)
        kraw, kinv = units(k_ref, h, hd)
        q = qraw * qinv * hd ** (-0.5)
        k = kraw * kinv
        last = sums[h][n - 1 : n, :]
        tail = jnp.exp(last - sums[h])
        grown = jnp.exp(sums[h])
        fade = jnp.where(i <= j, jnp.exp(jnp.where(i <= j, sum_rows[h] - sums[h], 0.0)), 0.0)
        state = s_ref[h]
        end = end_ref[h]
        ut_ref[h] = u_ref[h].T.astype(bf16)
        fade_ref[h] = fade
        sink_ref[h] = jnp.where(i < j, -fade * rows[h][1], 0.0)
        gram_ref[h] = mm(k, k, 1, 1)
        cross_ref[h] = mm(k, q, 1, 1)
        ks_ref[h] = grown * mm(k, state)
        qn_ref[h] = q.astype(bf16)
        kn_ref[h] = k.astype(bf16)
        dq_in = grown * mm(g_ref[:, h * hd : (h + 1) * hd], state, 1, 1)
        dk_in = -grown * mm(strengths[h] * z_ref[h], state, 1, 1)
        dq_ref[h] = dq_in
        dk_ref[h] = dk_in
        kend_ref[h] = tail * mm(k, end)
        sides.append(
            jnp.sum(q * dq_in, axis=1, keepdims=True) + jnp.sum(k * dk_in, axis=1, keepdims=True)
        )
        sides.append(tail)
        sides.append(strengths[h])
        total = jnp.exp(last) * jnp.sum(
            jnp.sum(state * end, axis=1, keepdims=True), axis=0, keepdims=True
        )
        sides.append(jnp.broadcast_to(total, (n, 1)))
    side_ref[...] = jnp.concatenate(sides, axis=1)


def kernel_gates(
    gates_ref,
    params_ref,
    tokens_ref,
    z_ref,
    ut_ref,
    fade_ref,
    sink_ref,
    gram_ref,
    cross_ref,
    ks_ref,
    kend_ref,
    side_ref,
    *refs,
    steps,
):
    g_ref = thirds(tokens_ref)[2]
    v_in = refs[:steps]
    gate_ref, small_ref, both_ref, new_ref, v_ref = refs[steps:]
    heads, n, hd = z_ref.shape
    me = place_level()
    block = n // steps
    for m in range(steps):
        at = pl.multiple_of((me ^ m) * block, block)
        v_ref[pl.ds(at, block), :] = v_in[m][...].astype(f32)
    i, j = positions(n)
    rows = gate_rows(gates_ref, params_ref, heads)
    side = side_ref[...]
    changes, products, sums, extra = [], [], [], []
    for h in range(heads):
        cols = slice(h * hd, (h + 1) * hd)
        base = side[:, 4 * h : 4 * h + 1]
        strength = side[:, 4 * h + 2 : 4 * h + 3]
        z = z_ref[h]
        new = mm(ut_ref[h], strength * (v_ref[:, cols] - ks_ref[h]))
        near = fade_ref[h] * mm(new, g_ref[:, cols], 1, 1)
        solve = sink_ref[h] * mm(new, z, 1, 1)
        both_ref[h, :, :n] = near.astype(bf16)
        both_ref[h, :, n:] = solve.astype(bf16)
        new_ref[h] = new.astype(bf16)
        pairs = near * cross_ref[h] + solve * gram_ref[h]
        weight = jnp.sum(new * kend_ref[h], axis=1, keepdims=True)
        changes.append(base - jnp.sum(pairs, axis=1, keepdims=True) - weight)
        products.append(jnp.sum(z * new, axis=1, keepdims=True))
        sums.append(jnp.sum(pairs, axis=0, keepdims=True))
        extra.append(jnp.sum(weight, axis=0, keepdims=True) + side[0:1, 4 * h + 3 : 4 * h + 4])
    from_rows = to_columns(sums)
    strength_rows = to_rows(products)
    si = lax.broadcasted_iota(jnp.int32, small_ref.shape, 0)
    sj = lax.broadcasted_iota(jnp.int32, small_ref.shape, 1)
    small = jnp.zeros(small_ref.shape, f32)
    for h in range(heads):
        change = changes[h] + from_rows[h]
        dlog = jnp.sum(jnp.where(i >= j, change, 0.0), axis=0, keepdims=True) + extra[h]
        dgate = dlog * rows[h][2]
        gate_ref[0, h : h + 1, :] = dgate
        gate_ref[1, h : h + 1, :] = strength_rows[h] * (1.0 - rows[h][1])
        first = jnp.sum(dlog * rows[h][0], axis=1, keepdims=True)
        second = jnp.sum(dgate, axis=1, keepdims=True)
        small = small + jnp.where((si == 0) & (sj == h), first, 0.0)
        small = small + jnp.where((si == 1) & (sj == h), second, 0.0)
    small_ref[...] = small


def kernel_units(
    tokens_ref, qn_ref, kn_ref, end_ref, dq_in_ref, dk_in_ref, side_ref, both_ref, new_ref, *outs
):
    dq_ref, dk_ref = outs
    q_ref, k_ref, _ = thirds(tokens_ref)
    heads, n, hd = new_ref.shape
    side = side_ref[...]
    for h in range(heads):
        cols = slice(h * hd, (h + 1) * hd)
        qraw, qinv = units(q_ref, h, hd)
        kraw, kinv = units(k_ref, h, hd)
        tail = side[:, 4 * h + 1 : 4 * h + 2]
        both = both_ref[h]
        by_key = mm(both, kn_ref[h], 0, 0)
        dq = by_key[:n] + dq_in_ref[h]
        dk = (
            mm(both[:, :n], qn_ref[h])
            + mm(both[:, n:], kn_ref[h])
            + by_key[n:]
            + dk_in_ref[h]
            + tail * mm(new_ref[h], end_ref[h], 1, 1)
        )
        dq = (hd ** (-0.5)) * (
            qinv * dq - qraw * (qinv * qinv * qinv * jnp.sum(qraw * dq, axis=1, keepdims=True))
        )
        dk = kinv * dk - kraw * (kinv * kinv * kinv * jnp.sum(kraw * dk, axis=1, keepdims=True))
        dq_ref[:, cols] = dq.astype(bf16)
        dk_ref[:, cols] = dk.astype(bf16)


def pieces(group):
    return sum(2 if m % 4 == 3 else 1 for m in group)


def pick(level, m, refs, scratch):
    if m % 4 != 3:
        return refs.pop(0)[...]
    straight, relayed = refs.pop(0), refs.pop(0)
    outer = (level + 1) % 4 < 2

    @pl.when(outer)
    def _():
        scratch[...] = relayed[...]

    @pl.when(jnp.logical_not(outer))
    def _():
        scratch[...] = straight[...]

    return scratch[...]


def kernel_values(*refs, chips, group):
    tokens = refs[:chips]
    chunks = pieces(group)
    mine = list(refs[chips : chips + chunks])
    theirs = list(refs[chips + chunks : chips + 2 * chunks])
    outs = refs[chips + 2 * chunks : -1]
    scratch = refs[-1]
    core = place_core()
    level = place_level()
    block = tokens[0].shape[0]
    part, width = mine[0].shape
    own_at = pl.multiple_of(core * part, part)
    other_at = pl.multiple_of((1 - core) * part, part)
    own = jnp.concatenate([ref[:, pl.ds(own_at, part)] for ref in tokens], axis=0)
    other = jnp.concatenate([ref[:, pl.ds(other_at, part)] for ref in tokens], axis=0)
    for m, number in enumerate(group):
        result = jnp.dot(
            own, pick(level, number, mine, scratch.at[0]), preferred_element_type=f32
        ) + jnp.dot(other, pick(level, number, theirs, scratch.at[1]), preferred_element_type=f32)
        for s in range(chips):
            outs[s][:, m * width : (m + 1) * width] = result[s * block : (s + 1) * block].astype(
                bf16
            )


def kernel_cut(tokens_hbm, *refs):
    outs, sems = refs[:-1], refs[-1]
    width = outs[0].shape[1]
    copies = []
    for s, out in enumerate(outs):
        at = pl.multiple_of((place_chip() ^ s) * width, width)
        copies.append(pltpu.make_async_copy(tokens_hbm.at[:, pl.ds(at, width)], out, sems.at[s]))
    for copy in copies:
        copy.start()
    for copy in copies:
        copy.wait()


def kernel_sum(*refs, chips):
    total = refs[0][...].astype(f32)
    for ref in refs[1:chips]:
        total = total + ref[...].astype(f32)
    outs = refs[chips:]
    width = outs[0].shape[1]
    for m, out_ref in enumerate(outs):
        out_ref[...] = total[:, m * width : (m + 1) * width].astype(out_ref.dtype)


def kernel_input(*refs, chips, group, first, final):
    grads = refs[:chips]
    chunks = pieces(group)
    mine = list(refs[chips : chips + chunks])
    theirs = list(refs[chips + chunks : chips + 2 * chunks])
    rest = list(refs[chips + 2 * chunks :])
    before = None if first else rest.pop(0)
    scratch = rest.pop()
    core = place_core()
    level = place_level()
    block = grads[0].shape[0]
    part, width = mine[0].shape
    rows = jnp.concatenate([ref[...] for ref in grads], axis=0)
    for index, (found, at) in enumerate(((mine, core * part), (theirs, (1 - core) * part))):
        total = None if first else before[index]
        for m in group:
            piece = lax.dot_general(
                rows[:, m * width : (m + 1) * width],
                pick(level, m, found, scratch.at[index]),
                (((1,), (1,)), ((), ())),
                preferred_element_type=f32,
            )
            total = piece if total is None else total + piece
        if final:
            place = pl.multiple_of(at, part)
            for s in range(chips):
                rest[s][:, pl.ds(place, part)] = total[s * block : (s + 1) * block].astype(bf16)
        else:
            rest[0][index] = total


def kernel_assemble(*refs):
    out_ref = refs[-1]
    width = refs[0].shape[1]
    me = place_chip()
    for s, ref in enumerate(refs[:-1]):
        at = pl.multiple_of((me ^ s) * width, width)
        out_ref[:, pl.ds(at, width)] = ref[...]


def kernel_join(*refs):
    out_ref = refs[-1]
    width = refs[0].shape[1]
    for m, ref in enumerate(refs[:-1]):
        out_ref[:, m * width : (m + 1) * width] = ref[...]


def kernel_decay(*refs):
    out_ref = refs[-1]
    total = functools.reduce(jnp.add, [ref[...] for ref in refs[:-1]])
    out_ref[...] = total[: out_ref.shape[0], : out_ref.shape[1]]


def struct(shape, kind):
    return jax.ShapeDtypeStruct(shape, kind)


VMEM = pl.BlockSpec(memory_space=pltpu.VMEM)
HBM = pl.BlockSpec(memory_space=pltpu.HBM)


def call(body, args, specs, outs, scratch=(), loads=()):
    specs = list(specs)
    grid = {}
    if loads:
        grid = dict(grid=(1,))
        for index in loads:
            shape = args[index].shape
            specs[index] = pl.BlockSpec(shape, lambda i, rank=len(shape): (0,) * rank)
    return pl.pallas_call(
        body,
        in_specs=specs,
        out_specs=[VMEM] * len(outs),
        out_shape=list(outs),
        scratch_shapes=list(scratch),
        cost_estimate=pl.CostEstimate(
            flops=3 * 10**9, bytes_accessed=20 * 10**6, transcendentals=0
        ),
        compiler_params=pltpu.CompilerParams(vmem_limit_bytes=12 * 1024 * 1024),
        **grid,
    )(*args)


def weight_order(steps):
    return sorted(range(1, steps), key=lambda m: (m // 4, (-m) % 2, m))


def per_device(
    layer_input, value_weight, query_raw, key_raw, out_grad, gate_logits, decay_params, saved_states
):
    plane = ("dp", "ctx")
    cores = 2
    blocks = lax.axis_size("ctx")
    members = lax.axis_size("dp") * blocks
    chips = members // cores
    steps = lax.axis_size("tp")
    tokens = layer_input[0]
    block, model = tokens.shape
    part, width = value_weight.shape
    hd = saved_states.shape[-1]
    heads = query_raw.shape[2] // hd
    length = query_raw.shape[1]
    q, k, g = query_raw[0], key_raw[0], out_grad[0]
    gates = gate_logits[:, 0]
    stacked = jnp.concatenate([q, k, g])
    states = saved_states[0, 0]

    def turn(array, m, places=None):
        pairs = [(t, t ^ m) for t in range(steps) if places is None or t in places]
        return lax.ppermute(array, "tp", pairs)

    def swap(array):
        return lax.ppermute(array, plane, [(p, p ^ 1) for p in range(members)])

    def cross(array, s):
        return lax.ppermute(array, plane, [(p, p ^ (cores * s)) for p in range(members)])

    mine = {0: (value_weight,)}
    for m in weight_order(steps):
        if m % 4 == 3:
            inner = [t for t in range(steps) if t % 4 in (1, 2)]
            straight = turn(value_weight, m, inner)
            relayed = turn(mine[m - 1][0], 1, inner)
            mine[m] = (straight, relayed)
        else:
            mine[m] = (turn(value_weight, m),)
    theirs = {m: tuple(swap(a) for a in mine[m]) for m in range(steps)}

    def chunks(found, group):
        return [a for m in group for a in found[m]]

    bc, x1, z0, inverse = call(
        kernel_a,
        (gates, decay_params, stacked),
        (VMEM, VMEM, VMEM),
        (
            struct((heads, hd, 2 * hd), bf16),
            struct((heads, length, hd), bf16),
            struct((heads, length, hd), f32),
            struct((heads, length, length), f32),
        ),
    )
    other = swap(bc)
    ranks = blocks // cores
    full = ranks > 2
    joined = call(
        functools.partial(kernel_compose, full=full),
        (bc, other),
        (VMEM, VMEM),
        (struct((heads, hd, hd), bf16),) + ((struct((heads, hd, 2 * hd), bf16),) if full else ()),
    )
    received = []
    for d in range(1, ranks):
        received.append(
            lax.ppermute(
                joined[1] if d < ranks - 1 else joined[0],
                "ctx",
                [(p, p - cores * d) for p in range(cores * d, blocks)],
            )
        )

    cuts = call(
        kernel_cut,
        (tokens,),
        (HBM,),
        tuple(struct((block, cores * part), bf16) for _ in range(chips)),
        scratch=(pltpu.SemaphoreType.DMA((chips,)),),
    )
    token_parts = [cuts[s] if s == 0 else cross(cuts[s], s) for s in range(chips)]

    outs = call(
        functools.partial(kernel_b, count=len(received), steps=steps),
        (gates, x1, z0, other, *received),
        (VMEM,) * (4 + len(received)),
        tuple(struct((block, width), bf16) for _ in range(steps))
        + (struct((heads, length, hd), f32), struct((heads, hd, hd), f32)),
        scratch=(pltpu.VMEM((length, width), f32),),
    )
    dv_blocks, z, end = outs[:steps], outs[steps], outs[steps + 1]
    dv_cols = [dv_blocks[m] if m == 0 else turn(dv_blocks[m], m) for m in range(steps)]
    dv_row = call(
        kernel_join, tuple(dv_cols), (VMEM,) * steps, (struct((block, steps * width), bf16),)
    )[0]
    dv_parts = [dv_row if s == 0 else cross(dv_row, s) for s in range(chips)]

    groups = [tuple(range(steps - 1)), (steps - 1,)]
    v_blocks = []
    for group in groups:
        sums = call(
            functools.partial(kernel_values, chips=chips, group=group),
            (*token_parts, *chunks(mine, group), *chunks(theirs, group)),
            (VMEM,) * (chips + 2 * len(chunks(mine, group))),
            tuple(struct((block, width * len(group)), bf16) for _ in range(chips)),
            scratch=(pltpu.VMEM((2, part, width), bf16),),
        )
        back = [sums[s] if s == 0 else cross(sums[s], s) for s in range(chips)]
        whole = call(
            functools.partial(kernel_sum, chips=chips),
            tuple(back),
            (VMEM,) * chips,
            tuple(struct((block, width), bf16) for _ in group),
        )
        v_blocks += [part_v if m == 0 else turn(part_v, m) for m, part_v in zip(group, whole)]

    acc = None
    for group in groups:
        first, final = group is groups[0], group is groups[-1]
        args = (*dv_parts, *chunks(mine, group), *chunks(theirs, group)) + (
            () if first else (acc,)
        )
        res = call(
            functools.partial(kernel_input, chips=chips, group=group, first=first, final=final),
            args,
            (VMEM,) * len(args),
            tuple(struct((block, cores * part), bf16) for _ in range(chips))
            if final
            else (struct((cores, chips * block, part), f32),),
            scratch=(pltpu.VMEM((2, part, width), bf16),),
        )
        if final:
            in_blocks = res
        else:
            acc = res[0]
    in_back = [in_blocks[s] if s == 0 else cross(in_blocks[s], s) for s in range(chips)]
    square = struct((heads, length, length), f32)
    tall = struct((heads, length, hd), f32)
    tall_half = struct((heads, length, hd), bf16)
    ut, fade, sink, gram, cross_prod, k_state, qn, kn, dq_in, dk_in, k_end, side = call(
        kernel_pre,
        (gates, decay_params, stacked, states, inverse, z, end),
        (VMEM,) * 7,
        (
            struct((heads, length, length), bf16),
            square,
            square,
            square,
            square,
            tall,
            tall_half,
            tall_half,
            tall,
            tall,
            tall,
            struct((length, 4 * heads), f32),
        ),
    )
    gate, small, both, new = call(
        functools.partial(kernel_gates, steps=steps),
        (
            gates,
            decay_params,
            stacked,
            z,
            ut,
            fade,
            sink,
            gram,
            cross_prod,
            k_state,
            k_end,
            side,
            *v_blocks,
        ),
        (VMEM,) * (12 + steps),
        (
            struct((2, heads, length), f32),
            struct((8, 128), f32),
            struct((heads, length, 2 * length), bf16),
            tall_half,
        ),
        scratch=(pltpu.VMEM((length, width), f32),),
    )
    dq, dk = call(
        kernel_units,
        (stacked, qn, kn, end, dq_in, dk_in, side, both, new),
        (VMEM,) * 9,
        (struct((length, width), bf16), struct((length, width), bf16)),
    )
    tile = (struct(small.shape, f32),)
    small = call(kernel_decay, (small, swap(small)), (VMEM, VMEM), tile)[0]
    input_grad = call(
        kernel_assemble, tuple(in_back), (VMEM,) * chips, (struct((block, model), bf16),)
    )[0]
    shares = [small if s == 0 else cross(small, s) for s in range(chips)]
    decay_grad = call(kernel_decay, tuple(shares), (VMEM,) * chips, (struct((2, heads), f32),))[0]
    return (input_grad[None], dq[None], dk[None], gate[:, None], decay_grad)


def solution(mesh):
    placed = (
        P("dp", ("ctx", "tp"), None),
        P(("dp", "ctx"), "tp"),
        P("dp", "ctx", "tp"),
        P("dp", "ctx", "tp"),
        P("dp", "ctx", "tp"),
        P(None, "dp", "tp", "ctx"),
        P(None, "tp"),
        P("dp", "ctx", "tp", None, None),
    )
    return jax.shard_map(
        per_device,
        mesh=mesh,
        in_specs=placed,
        out_specs=(
            P("dp", ("ctx", "tp"), None),
            P("dp", "ctx", "tp"),
            P("dp", "ctx", "tp"),
            P(None, "dp", "tp", "ctx"),
            P(None, "tp"),
        ),
        check_vma=False,
    )
```

profile of v0, /device:TPU:0, one launch (start us, length us, event | category | flops | bytes accessed | tf_op | source)
XLA Modules:
  0.0 105.0 jit_solution(13331590795404266950)
XLA Ops:
  3.1 4.3 %shard_map.119 = (bf16[2,128,256]{2,1,0:T(8,128)(2,1)S(1)}, bf16[2,256,128]{2,1,0:T(8,128)(2,1)S(1)}, f32[2,256,128]{2,1,0:T(8,128)S(1)}, f32[2,256,256]{2,1,0:T(8,128)S(1)}) custom-call(f32[2,2,256]{2,1,0:T(2,128)S(1)} %bitcast.14, f32[2,2]{1,0:T(2,128)S(1)} %copy-done.5, bf16[768,256]{1,0:T(8,128)(2,1)S(1)} %pad_maximum_fusion.tokens_ref), custom_call_target="tpu_custom_call" | custom-call | flops 3000000000 | bytes 20000000 | tf_op jit(solution)/shard_map/pallas_call | solution.py:538
  8.0 2.6 %collective-permute-start.13 = (bf16[1024,256]{1,0:T(8,128)(2,1)S(1)}, bf16[1024,256]{1,0:T(8,128)(2,1)S(1)}, u32[]{:S(2)}, u32[]{:S(2)}) collective-permute-start(bf16[1024,256]{1,0:T(8,128)(2,1)S(1)} %copy-done.1), channel_id=1, source_target_pairs={{0,1},{1,0},{2,3},{3,2},{4,5},{5,4},{6,7},{7,6},{8,9},{9,8},{10,11... | collective-permute-start | bytes 1572872 | tf_op jit(solution)/shard_map/ppermute | solution.py:578
  10.6 2.6 %collective-permute-start.9 = (bf16[1024,256]{1,0:T(8,128)(2,1)S(1)}, bf16[1024,256]{1,0:T(8,128)(2,1)S(1)}, u32[]{:S(2)}, u32[]{:S(2)}) collective-permute-start(bf16[1024,256]{1,0:T(8,128)(2,1)S(1)} %copy-done.1), channel_id=1, source_target_pairs={{0,2},{1,3},{2,0},{3,1},{4,6},{5,7},{6,4},{7,5},{8,10},{9,11},{10,... | collective-permute-start | bytes 1572872 | tf_op jit(solution)/shard_map/ppermute | solution.py:578
  13.4 1.3 %collective-permute-start.1 = (bf16[2,128,128]{2,1,0:T(8,128)(2,1)S(1)}, bf16[2,128,128]{2,1,0:T(8,128)(2,1)S(1)}, u32[]{:S(2)}, u32[]{:S(2)}) collective-permute-start(bf16[2,128,128]{2,1,0:T(8,128)(2,1)S(1)} %shard_map.120), channel_id=1, source_target_pairs={{8,0},{12,4},{9,1},{13,5},{10,2},{14,6},{11,3},{15,7},{24,16},{28,... | collective-permute-start | bytes 196616 | tf_op jit(solution)/shard_map/ppermute | solution.py:623
  14.8 2.7 %collective-permute-start.20 = (bf16[64,2048]{1,0:T(8,128)(2,1)S(1)}, bf16[64,2048]{1,0:T(8,128)(2,1)S(1)}, u32[]{:S(2)}, u32[]{:S(2)}) collective-permute-start(bf16[64,2048]{1,0:T(8,128)(2,1)S(1)} %get-tuple-element.79), channel_id=1, source_target_pairs={{0,8},{4,12},{8,0},{12,4},{16,24},{20,28},{24,16},{28,20},{1,9},{5... | collective-permute-start | bytes 786440 | tf_op jit(solution)/shard_map/ppermute | solution.py:584
  17.6 2.7 %collective-permute-done.1.refs_0_ = bf16[2,128,128]{2,1,0:T(8,128)(2,1)S(1)} collective-permute-done((bf16[2,128,128]{2,1,0:T(8,128)(2,1)S(1)}, bf16[2,128,128]{2,1,0:T(8,128)(2,1)S(1)}, u32[]{:S(2)}, u32[]{:S(2)}) %collective-permute-start.1) | collective-permute-done | bytes 65568 | tf_op jit(solution)/shard_map/ppermute | solution.py:623
  21.9 13.0 %collective-permute-done.2.refs_1_ = bf16[64,256]{1,0:T(8,128)(2,1)S(1)} collective-permute-done((bf16[64,256]{1,0:T(8,128)(2,1)S(1)}, bf16[64,256]{1,0:T(8,128)(2,1)S(1)}, u32[]{:S(2)}, u32[]{:S(2)}) %collective-permute-start.2) | collective-permute-done | bytes 32800 | tf_op jit(solution)/shard_map/ppermute | solution.py:578
  34.9 2.7 %collective-permute-start.4 = (bf16[64,256]{1,0:T(8,128)(2,1)S(1)}, bf16[64,256]{1,0:T(8,128)(2,1)S(1)}, u32[]{:S(2)}, u32[]{:S(2)}) collective-permute-start(bf16[64,256]{1,0:T(8,128)(2,1)S(1)} %get-tuple-element.58), channel_id=1, source_target_pairs={{0,3},{1,2},{2,1},{3,0},{4,7},{5,6},{6,5},{7,4},{8,11},{9,10},{10,... | collective-permute-start | bytes 98312 | tf_op jit(solution)/shard_map/ppermute | solution.py:578
  38.2 1.5 %collective-permute-start.21 = (bf16[64,2048]{1,0:T(8,128)(2,1)S(1)}, bf16[64,2048]{1,0:T(8,128)(2,1)S(1)}, u32[]{:S(2)}, u32[]{:S(2)}) collective-permute-start(bf16[64,2048]{1,0:T(8,128)(2,1)S(1)} %get-tuple-element.80), channel_id=1, source_target_pairs={{0,16},{4,20},{8,24},{12,28},{16,0},{20,4},{24,8},{28,12},{1,17},{... | collective-permute-start | bytes 786440 | tf_op jit(solution)/shard_map/ppermute | solution.py:584
  40.8 2.6 %collective-permute-start.22 = (bf16[64,2048]{1,0:T(8,128)(2,1)S(1)}, bf16[64,2048]{1,0:T(8,128)(2,1)S(1)}, u32[]{:S(2)}, u32[]{:S(2)}) collective-permute-start(bf16[64,2048]{1,0:T(8,128)(2,1)S(1)} %get-tuple-element.81), channel_id=1, source_target_pairs={{0,24},{4,28},{8,16},{12,20},{16,8},{20,12},{24,0},{28,4},{1,25},{... | collective-permute-start | bytes 786440 | tf_op jit(solution)/shard_map/ppermute | solution.py:584
  44.1 1.3 %collective-permute-start.10 = (bf16[1024,256]{1,0:T(8,128)(2,1)S(1)}, bf16[1024,256]{1,0:T(8,128)(2,1)S(1)}, u32[]{:S(2)}, u32[]{:S(2)}) collective-permute-start(bf16[1024,256]{1,0:T(8,128)(2,1)S(1)} %collective-permute-done.9.refs_6_), channel_id=1, source_target_pairs={{1,0},{2,3},{5,4},{6,7},{9,8},{10,11},{13,12},{14,15},{17,16},{18,... | collective-permute-start | bytes 1572872 | tf_op jit(solution)/shard_map/ppermute | solution.py:578
  45.4 2.0 %collective-permute-done.21.refs_2_ = bf16[64,2048]{1,0:T(8,128)(2,1)S(1)} collective-permute-done((bf16[64,2048]{1,0:T(8,128)(2,1)S(1)}, bf16[64,2048]{1,0:T(8,128)(2,1)S(1)}, u32[]{:S(2)}, u32[]{:S(2)}) %collective-permute-start.21) | collective-permute-done | bytes 262176 | tf_op jit(solution)/shard_map/ppermute | solution.py:584
  47.3 4.3 %collective-permute-done.22.refs_3_ = bf16[64,2048]{1,0:T(8,128)(2,1)S(1)} collective-permute-done((bf16[64,2048]{1,0:T(8,128)(2,1)S(1)}, bf16[64,2048]{1,0:T(8,128)(2,1)S(1)}, u32[]{:S(2)}, u32[]{:S(2)}) %collective-permute-start.22) | collective-permute-done | bytes 262176 | tf_op jit(solution)/shard_map/ppermute | solution.py:584
  52.2 1.5 %shard_map.126 = (bf16[2,256,256]{2,1,0:T(8,128)(2,1)S(1)}, f32[2,256,256]{2,1,0:T(8,128)S(1)}, f32[2,256,256]{2,1,0:T(8,128)S(1)}, f32[2,256,256]{2,1,0:T(8,128...) custom-call(f32[2,2,256]{2,1,0:T(2,128)S(1)} %bitcast.16, ...), custom_call_target="tpu_custom_call" | custom-call | flops 3000000000 | bytes 20000000 | tf_op jit(solution)/shard_map/pallas_call | solution.py:538
  53.8 4.2 %collective-permute-done.10.refs_5_ = bf16[1024,256]{1,0:T(8,128)(2,1)S(1)} collective-permute-done((bf16[1024,256]{1,0:T(8,128)(2,1)S(1)}, bf16[1024,256]{1,0:T(8,128)(2,1)S(1)}, u32[]{:S(2)}, u32[]{:S(2)}) %collective-permute-start.10) | collective-permute-done | bytes 524320 | tf_op jit(solution)/shard_map/ppermute | solution.py:578
  58.5 1.5 %collective-permute-start.6 = (bf16[64,1024]{1,0:T(8,128)(2,1)S(1)}, bf16[64,1024]{1,0:T(8,128)(2,1)S(1)}, u32[]{:S(2)}, u32[]{:S(2)}) collective-permute-start(bf16[64,1024]{1,0:T(8,128)(2,1)S(1)} %shard_map.122.refs_0_), channel_id=1, source_target_pairs={{0,16},{4,20},{8,24},{12,28},{16,0},{20,4},{24,8},{28,12},{1,17},{... | collective-permute-start | bytes 393224 | tf_op jit(solution)/shard_map/ppermute | solution.py:584
  61.0 1.6 %collective-permute-start.23 = (bf16[64,768]{1,0:T(8,128)(2,1)S(1)}, bf16[64,768]{1,0:T(8,128)(2,1)S(1)}, u32[]{:S(2)}, u32[]{:S(2)}) collective-permute-start(bf16[64,768]{1,0:T(8,128)(2,1)S(1)} %get-tuple-element.83), channel_id=1, source_target_pairs={{0,8},{4,12},{8,0},{12,4},{16,24},{20,28},{24,16},{28,20},{1,9},{5... | collective-permute-start | bytes 294920 | tf_op jit(solution)/shard_map/ppermute | solution.py:584
  63.1 1.5 %collective-permute-start.25 = (bf16[64,768]{1,0:T(8,128)(2,1)S(1)}, bf16[64,768]{1,0:T(8,128)(2,1)S(1)}, u32[]{:S(2)}, u32[]{:S(2)}) collective-permute-start(bf16[64,768]{1,0:T(8,128)(2,1)S(1)} %get-tuple-element.85), channel_id=1, source_target_pairs={{0,24},{4,28},{8,16},{12,20},{16,8},{20,12},{24,0},{28,4},{1,25},{... | collective-permute-start | bytes 294920 | tf_op jit(solution)/shard_map/ppermute | solution.py:584
  65.2 1.8 %collective-permute-done.23.refs_1_ = bf16[64,768]{1,0:T(8,128)(2,1)S(1)} collective-permute-done((bf16[64,768]{1,0:T(8,128)(2,1)S(1)}, bf16[64,768]{1,0:T(8,128)(2,1)S(1)}, u32[]{:S(2)}, u32[]{:S(2)}) %collective-permute-start.23) | collective-permute-done | bytes 98336 | tf_op jit(solution)/shard_map/ppermute | solution.py:584
  67.6 1.7 %collective-permute-done.24.refs_2_ = bf16[64,768]{1,0:T(8,128)(2,1)S(1)} collective-permute-done((bf16[64,768]{1,0:T(8,128)(2,1)S(1)}, bf16[64,768]{1,0:T(8,128)(2,1)S(1)}, u32[]{:S(2)}, u32[]{:S(2)}) %collective-permute-start.24) | collective-permute-done | bytes 98336 | tf_op jit(solution)/shard_map/ppermute | solution.py:584
  69.8 2.2 %collective-permute-done.25.refs_3_ = bf16[64,768]{1,0:T(8,128)(2,1)S(1)} collective-permute-done((bf16[64,768]{1,0:T(8,128)(2,1)S(1)}, bf16[64,768]{1,0:T(8,128)(2,1)S(1)}, u32[]{:S(2)}, u32[]{:S(2)}) %collective-permute-start.25) | collective-permute-done | bytes 98336 | tf_op jit(solution)/shard_map/ppermute | solution.py:584
  72.5 1.6 %collective-permute-start.5 = (bf16[64,1024]{1,0:T(8,128)(2,1)S(1)}, bf16[64,1024]{1,0:T(8,128)(2,1)S(1)}, u32[]{:S(2)}, u32[]{:S(2)}) collective-permute-start(bf16[64,1024]{1,0:T(8,128)(2,1)S(1)} %shard_map.122.refs_0_), channel_id=1, source_target_pairs={{0,8},{4,12},{8,0},{12,4},{16,24},{20,28},{24,16},{28,20},{1,9},{5... | collective-permute-start | bytes 393224 | tf_op jit(solution)/shard_map/ppermute | solution.py:584
  74.1 2.8 %collective-permute-done.30.refs_3_ = bf16[64,256]{1,0:T(8,128)(2,1)S(1)} collective-permute-done((bf16[64,256]{1,0:T(8,128)(2,1)S(1)}, bf16[64,256]{1,0:T(8,128)(2,1)S(1)}, u32[]{:S(2)}, u32[]{:S(2)}) %collective-permute-start.30) | collective-permute-done | bytes 32800 | tf_op jit(solution)/shard_map/ppermute | solution.py:584
  77.4 2.0 %collective-permute-start.31 = (bf16[64,256]{1,0:T(8,128)(2,1)S(1)}, bf16[64,256]{1,0:T(8,128)(2,1)S(1)}, u32[]{:S(2)}, u32[]{:S(2)}) collective-permute-start(bf16[64,256]{1,0:T(8,128)(2,1)S(1)} %shard_map.131), channel_id=1, source_target_pairs={{0,3},{1,2},{2,1},{3,0},{4,7},{5,6},{6,5},{7,4},{8,11},{9,10},{10,... | collective-permute-start | bytes 98312 | tf_op jit(solution)/shard_map/ppermute | solution.py:578
  80.4 1.3 %collective-permute-done.27.refs_2_ = bf16[64,256]{1,0:T(8,128)(2,1)S(1)} collective-permute-done((bf16[64,256]{1,0:T(8,128)(2,1)S(1)}, bf16[64,256]{1,0:T(8,128)(2,1)S(1)}, u32[]{:S(2)}, u32[]{:S(2)}) %collective-permute-start.27) | collective-permute-done | bytes 32800 | tf_op jit(solution)/shard_map/ppermute | solution.py:578
  81.7 1.5 %collective-permute-done.31.refs_3_ = bf16[64,256]{1,0:T(8,128)(2,1)S(1)} collective-permute-done((bf16[64,256]{1,0:T(8,128)(2,1)S(1)}, bf16[64,256]{1,0:T(8,128)(2,1)S(1)}, u32[]{:S(2)}, u32[]{:S(2)}) %collective-permute-start.31) | collective-permute-done | bytes 32800 | tf_op jit(solution)/shard_map/ppermute | solution.py:578
  83.2 1.7 %shard_map.132 = (f32[2,2,256]{2,1,0:T(2,128)}, f32[8,128]{1,0:T(8,128)S(1)}, bf16[2,256,512]{2,1,0:T(8,128)(2,1)S(1)}, bf16[2,256,128]{2,1,0:T(8,128)(2,1)S(1)}) custom-call(f32[2,2,256]{2,1,0:T(2,128)S(1)} %bitcast.17, f32[2,2]{1,0:T(2,128)S(1)} %copy-done.6, bf16[768,256]{1,0:T(8,128)(2,1)S(1)} %pad_maximum_fusion.tokens_ref, ...), custom_call_target="tpu_custom_call" | custom-call | flops 3000000000 | bytes 20000000 | tf_op jit(solution)/shard_map/pallas_call | solution.py:538
  86.3 1.2 %collective-permute-start.18 = (bf16[64,2048]{1,0:T(8,128)(2,1)S(1)}, bf16[64,2048]{1,0:T(8,128)(2,1)S(1)}, u32[]{:S(2)}, u32[]{:S(2)}) collective-permute-start(bf16[64,2048]{1,0:T(8,128)(2,1)S(1)} %get-tuple-element.61), channel_id=1, source_target_pairs={{0,16},{4,20},{8,24},{12,28},{16,0},{20,4},{24,8},{28,12},{1,17},{... | collective-permute-start | bytes 786440 | tf_op jit(solution)/shard_map/ppermute | solution.py:584
  87.5 1.8 %collective-permute-start.35 = (f32[8,128]{1,0:T(8,128)S(1)}, f32[8,128]{1,0:T(8,128)S(1)}, u32[]{:S(2)}, u32[]{:S(2)}) collective-permute-start(f32[8,128]{1,0:T(8,128)S(1)} %shard_map.134.refs_0_), channel_id=1, source_target_pairs={{0,24},{4,28},{8,16},{12,20},{16,8},{20,12},{24,0},{28,4},{1,25},{... | collective-permute-start | bytes 12296 | tf_op jit(solution)/shard_map/ppermute | solution.py:584
  90.9 1.5 %shard_map.133 = (bf16[256,256]{1,0:T(8,128)(2,1)}, bf16[256,256]{1,0:T(8,128)(2,1)}) custom-call(bf16[768,256]{1,0:T(8,128)(2,1)S(1)} %pad_maximum_fusion.tokens_ref, bf16[2,256,128]{2,1,0:T(8,128)(2,1)S(1)} %get-tuple-element.66.qn_ref, bf16[2,256,128]{2,1,0:T(8,128)(2,1)S(1)} %get-tuple-element.67.kn_ref, f32[2,128,128]{2,1,0:T(8,128)S(1)} %get-tuple-element.65.end_ref, ...), custom_call_target="tpu_custom_call" | custom-call | flops 3000000000 | bytes 20000000 | tf_op jit(solution)/shard_map/pallas_call | solution.py:538
  92.4 3.4 %collective-permute-done.35.refs_3_ = f32[8,128]{1,0:T(8,128)S(1)} collective-permute-done((f32[8,128]{1,0:T(8,128)S(1)}, f32[8,128]{1,0:T(8,128)S(1)}, u32[]{:S(2)}, u32[]{:S(2)}) %collective-permute-start.35) | collective-permute-done | bytes 4128 | tf_op jit(solution)/shard_map/ppermute | solution.py:584
  97.5 6.5 %collective-permute-done.19.refs_3_ = bf16[64,2048]{1,0:T(8,128)(2,1)S(1)} collective-permute-done((bf16[64,2048]{1,0:T(8,128)(2,1)S(1)}, bf16[64,2048]{1,0:T(8,128)(2,1)S(1)}, u32[]{:S(2)}, u32[]{:S(2)}) %collective-permute-start.19) | collective-permute-done | bytes 262176 | tf_op jit(solution)/shard_map/ppermute | solution.py:584
  (72 shorter events, 19.6 us)
Async XLA Ops:
  7.4 5.8 %collective-permute-start = (bf16[2,128,256]{2,1,0:T(8,128)(2,1)S(1)}, bf16[2,128,256]{2,1,0:T(8,128)(2,1)S(1)}, u32[]{:S(2)}, u32[]{:S(2)}) collective-permute-start(bf16[2,128,256]{2,1,0:T(8,128)(2,1)S(1)} %get-tuple-element.54.bc_ref), channel_id=1, source_target_pairs={{0,4},{4,0},{8,12},{12,8},{16,20},{20,16},{24,28},{28,24},{1,5},{5... | collective-permute-start | bytes 393224 | tf_op jit(solution)/shard_map/ppermute | solution.py:581
  8.0 43.7 %collective-permute-start.13 = (bf16[1024,256]{1,0:T(8,128)(2,1)S(1)}, bf16[1024,256]{1,0:T(8,128)(2,1)S(1)}, u32[]{:S(2)}, u32[]{:S(2)}) collective-permute-start(bf16[1024,256]{1,0:T(8,128)(2,1)S(1)} %copy-done.1), channel_id=1, source_target_pairs={{0,1},{1,0},{2,3},{3,2},{4,5},{5,4},{6,7},{7,6},{8,9},{9,8},{10,11... | collective-permute-start | bytes 1572872 | tf_op jit(solution)/shard_map/ppermute | solution.py:578
  10.6 33.4 %collective-permute-start.9 = (bf16[1024,256]{1,0:T(8,128)(2,1)S(1)}, bf16[1024,256]{1,0:T(8,128)(2,1)S(1)}, u32[]{:S(2)}, u32[]{:S(2)}) collective-permute-start(bf16[1024,256]{1,0:T(8,128)(2,1)S(1)} %copy-done.1), channel_id=1, source_target_pairs={{0,2},{1,3},{2,0},{3,1},{4,6},{5,7},{6,4},{7,5},{8,10},{9,11},{10,... | collective-permute-start | bytes 1572872 | tf_op jit(solution)/shard_map/ppermute | solution.py:578
  13.4 6.9 %collective-permute-start.1 = (bf16[2,128,128]{2,1,0:T(8,128)(2,1)S(1)}, bf16[2,128,128]{2,1,0:T(8,128)(2,1)S(1)}, u32[]{:S(2)}, u32[]{:S(2)}) collective-permute-start(bf16[2,128,128]{2,1,0:T(8,128)(2,1)S(1)} %shard_map.120), channel_id=1, source_target_pairs={{8,0},{12,4},{9,1},{13,5},{10,2},{14,6},{11,3},{15,7},{24,16},{28,... | collective-permute-start | bytes 196616 | tf_op jit(solution)/shard_map/ppermute | solution.py:623
  14.8 28.5 %collective-permute-start.20 = (bf16[64,2048]{1,0:T(8,128)(2,1)S(1)}, bf16[64,2048]{1,0:T(8,128)(2,1)S(1)}, u32[]{:S(2)}, u32[]{:S(2)}) collective-permute-start(bf16[64,2048]{1,0:T(8,128)(2,1)S(1)} %get-tuple-element.79), channel_id=1, source_target_pairs={{0,8},{4,12},{8,0},{12,4},{16,24},{20,28},{24,16},{28,20},{1,9},{5... | collective-permute-start | bytes 786440 | tf_op jit(solution)/shard_map/ppermute | solution.py:584
  20.6 14.3 %collective-permute-start.2 = (bf16[64,256]{1,0:T(8,128)(2,1)S(1)}, bf16[64,256]{1,0:T(8,128)(2,1)S(1)}, u32[]{:S(2)}, u32[]{:S(2)}) collective-permute-start(bf16[64,256]{1,0:T(8,128)(2,1)S(1)} %get-tuple-element.56), channel_id=1, source_target_pairs={{0,1},{1,0},{2,3},{3,2},{4,5},{5,4},{6,7},{7,6},{8,9},{9,8},{10,11... | collective-permute-start | bytes 98312 | tf_op jit(solution)/shard_map/ppermute | solution.py:578
  21.1 17.0 %collective-permute-start.3 = (bf16[64,256]{1,0:T(8,128)(2,1)S(1)}, bf16[64,256]{1,0:T(8,128)(2,1)S(1)}, u32[]{:S(2)}, u32[]{:S(2)}) collective-permute-start(bf16[64,256]{1,0:T(8,128)(2,1)S(1)} %get-tuple-element.57), channel_id=1, source_target_pairs={{0,2},{1,3},{2,0},{3,1},{4,6},{5,7},{6,4},{7,5},{8,10},{9,11},{10,... | collective-permute-start | bytes 98312 | tf_op jit(solution)/shard_map/ppermute | solution.py:578
  34.9 5.8 %collective-permute-start.4 = (bf16[64,256]{1,0:T(8,128)(2,1)S(1)}, bf16[64,256]{1,0:T(8,128)(2,1)S(1)}, u32[]{:S(2)}, u32[]{:S(2)}) collective-permute-start(bf16[64,256]{1,0:T(8,128)(2,1)S(1)} %get-tuple-element.58), channel_id=1, source_target_pairs={{0,3},{1,2},{2,1},{3,0},{4,7},{5,6},{6,5},{7,4},{8,11},{9,10},{10,... | collective-permute-start | bytes 98312 | tf_op jit(solution)/shard_map/ppermute | solution.py:578
  38.2 9.2 %collective-permute-start.21 = (bf16[64,2048]{1,0:T(8,128)(2,1)S(1)}, bf16[64,2048]{1,0:T(8,128)(2,1)S(1)}, u32[]{:S(2)}, u32[]{:S(2)}) collective-permute-start(bf16[64,2048]{1,0:T(8,128)(2,1)S(1)} %get-tuple-element.80), channel_id=1, source_target_pairs={{0,16},{4,20},{8,24},{12,28},{16,0},{20,4},{24,8},{28,12},{1,17},{... | collective-permute-start | bytes 786440 | tf_op jit(solution)/shard_map/ppermute | solution.py:584
  40.8 10.9 %collective-permute-start.22 = (bf16[64,2048]{1,0:T(8,128)(2,1)S(1)}, bf16[64,2048]{1,0:T(8,128)(2,1)S(1)}, u32[]{:S(2)}, u32[]{:S(2)}) collective-permute-start(bf16[64,2048]{1,0:T(8,128)(2,1)S(1)} %get-tuple-element.81), channel_id=1, source_target_pairs={{0,24},{4,28},{8,16},{12,20},{16,8},{20,12},{24,0},{28,4},{1,25},{... | collective-permute-start | bytes 786440 | tf_op jit(solution)/shard_map/ppermute | solution.py:584
  43.4 10.3 %collective-permute-start.8 = (bf16[1024,256]{1,0:T(8,128)(2,1)S(1)}, bf16[1024,256]{1,0:T(8,128)(2,1)S(1)}, u32[]{:S(2)}, u32[]{:S(2)}) collective-permute-start(bf16[1024,256]{1,0:T(8,128)(2,1)S(1)} %copy-done.1), channel_id=1, source_target_pairs={{1,2},{2,1},{5,6},{6,5},{9,10},{10,9},{13,14},{14,13},{17,18},{18,... | collective-permute-start | bytes 1572872 | tf_op jit(solution)/shard_map/ppermute | solution.py:578
  44.1 13.9 %collective-permute-start.10 = (bf16[1024,256]{1,0:T(8,128)(2,1)S(1)}, bf16[1024,256]{1,0:T(8,128)(2,1)S(1)}, u32[]{:S(2)}, u32[]{:S(2)}) collective-permute-start(bf16[1024,256]{1,0:T(8,128)(2,1)S(1)} %collective-permute-done.9.refs_6_), channel_id=1, source_target_pairs={{1,0},{2,3},{5,4},{6,7},{9,8},{10,11},{13,12},{14,15},{17,16},{18,... | collective-permute-start | bytes 1572872 | tf_op jit(solution)/shard_map/ppermute | solution.py:578
  47.3 10.6 %collective-permute-start.14 = (bf16[1024,256]{1,0:T(8,128)(2,1)S(1)}, bf16[1024,256]{1,0:T(8,128)(2,1)S(1)}, u32[]{:S(2)}, u32[]{:S(2)}) collective-permute-start(bf16[1024,256]{1,0:T(8,128)(2,1)S(1)} %copy-done.1), channel_id=1, source_target_pairs={{0,4},{4,0},{8,12},{12,8},{16,20},{20,16},{24,28},{28,24},{1,5},{5... | collective-permute-start | bytes 1572872 | tf_op jit(solution)/shard_map/ppermute | solution.py:581
  51.7 8.3 %collective-permute-start.16 = (bf16[1024,256]{1,0:T(8,128)(2,1)S(1)}, bf16[1024,256]{1,0:T(8,128)(2,1)S(1)}, u32[]{:S(2)}, u32[]{:S(2)}) collective-permute-start(bf16[1024,256]{1,0:T(8,128)(2,1)S(1)} %collective-permute-done.9.refs_6_), channel_id=1, source_target_pairs={{0,4},{4,0},{8,12},{12,8},{16,20},{20,16},{24,28},{28,24},{1,5},{5... | collective-permute-start | bytes 1572872 | tf_op jit(solution)/shard_map/ppermute | solution.py:581
  51.7 6.8 %collective-permute-start.15 = (bf16[1024,256]{1,0:T(8,128)(2,1)S(1)}, bf16[1024,256]{1,0:T(8,128)(2,1)S(1)}, u32[]{:S(2)}, u32[]{:S(2)}) collective-permute-start(bf16[1024,256]{1,0:T(8,128)(2,1)S(1)} %collective-permute-done.13.refs_5_), channel_id=1, source_target_pairs={{0,4},{4,0},{8,12},{12,8},{16,20},{20,16},{24,28},{28,24},{1,5},{5... | collective-permute-start | bytes 1572872 | tf_op jit(solution)/shard_map/ppermute | solution.py:581
  53.7 8.9 %collective-permute-start.11 = (bf16[1024,256]{1,0:T(8,128)(2,1)S(1)}, bf16[1024,256]{1,0:T(8,128)(2,1)S(1)}, u32[]{:S(2)}, u32[]{:S(2)}) collective-permute-start(bf16[1024,256]{1,0:T(8,128)(2,1)S(1)} %collective-permute-done.8.refs_4_), channel_id=1, source_target_pairs={{0,4},{4,0},{8,12},{12,8},{16,20},{20,16},{24,28},{28,24},{1,5},{5... | collective-permute-start | bytes 1572872 | tf_op jit(solution)/shard_map/ppermute | solution.py:581
  57.9 5.2 %collective-permute-start.12 = (bf16[1024,256]{1,0:T(8,128)(2,1)S(1)}, bf16[1024,256]{1,0:T(8,128)(2,1)S(1)}, u32[]{:S(2)}, u32[]{:S(2)}) collective-permute-start(bf16[1024,256]{1,0:T(8,128)(2,1)S(1)} %collective-permute-done.10.refs_5_), channel_id=1, source_target_pairs={{0,4},{4,0},{8,12},{12,8},{16,20},{20,16},{24,28},{28,24},{1,5},{5... | collective-permute-start | bytes 1572872 | tf_op jit(solution)/shard_map/ppermute | solution.py:581
  58.0 19.4 %collective-permute-start.7 = (bf16[64,1024]{1,0:T(8,128)(2,1)S(1)}, bf16[64,1024]{1,0:T(8,128)(2,1)S(1)}, u32[]{:S(2)}, u32[]{:S(2)}) collective-permute-start(bf16[64,1024]{1,0:T(8,128)(2,1)S(1)} %shard_map.122.refs_0_), channel_id=1, source_target_pairs={{0,24},{4,28},{8,16},{12,20},{16,8},{20,12},{24,0},{28,4},{1,25},{... | collective-permute-start | bytes 393224 | tf_op jit(solution)/shard_map/ppermute | solution.py:584
  58.5 20.9 %collective-permute-start.6 = (bf16[64,1024]{1,0:T(8,128)(2,1)S(1)}, bf16[64,1024]{1,0:T(8,128)(2,1)S(1)}, u32[]{:S(2)}, u32[]{:S(2)}) collective-permute-start(bf16[64,1024]{1,0:T(8,128)(2,1)S(1)} %shard_map.122.refs_0_), channel_id=1, source_target_pairs={{0,16},{4,20},{8,24},{12,28},{16,0},{20,4},{24,8},{28,12},{1,17},{... | collective-permute-start | bytes 393224 | tf_op jit(solution)/shard_map/ppermute | solution.py:584
  61.0 5.9 %collective-permute-start.23 = (bf16[64,768]{1,0:T(8,128)(2,1)S(1)}, bf16[64,768]{1,0:T(8,128)(2,1)S(1)}, u32[]{:S(2)}, u32[]{:S(2)}) collective-permute-start(bf16[64,768]{1,0:T(8,128)(2,1)S(1)} %get-tuple-element.83), channel_id=1, source_target_pairs={{0,8},{4,12},{8,0},{12,4},{16,24},{20,28},{24,16},{28,20},{1,9},{5... | collective-permute-start | bytes 294920 | tf_op jit(solution)/shard_map/ppermute | solution.py:584
  62.6 6.7 %collective-permute-start.24 = (bf16[64,768]{1,0:T(8,128)(2,1)S(1)}, bf16[64,768]{1,0:T(8,128)(2,1)S(1)}, u32[]{:S(2)}, u32[]{:S(2)}) collective-permute-start(bf16[64,768]{1,0:T(8,128)(2,1)S(1)} %get-tuple-element.84), channel_id=1, source_target_pairs={{0,16},{4,20},{8,24},{12,28},{16,0},{20,4},{24,8},{28,12},{1,17},{... | collective-permute-start | bytes 294920 | tf_op jit(solution)/shard_map/ppermute | solution.py:584
  63.1 8.8 %collective-permute-start.25 = (bf16[64,768]{1,0:T(8,128)(2,1)S(1)}, bf16[64,768]{1,0:T(8,128)(2,1)S(1)}, u32[]{:S(2)}, u32[]{:S(2)}) collective-permute-start(bf16[64,768]{1,0:T(8,128)(2,1)S(1)} %get-tuple-element.85), channel_id=1, source_target_pairs={{0,24},{4,28},{8,16},{12,20},{16,8},{20,12},{24,0},{28,4},{1,25},{... | collective-permute-start | bytes 294920 | tf_op jit(solution)/shard_map/ppermute | solution.py:584
  66.9 5.6 %collective-permute-start.28 = (bf16[64,256]{1,0:T(8,128)(2,1)S(1)}, bf16[64,256]{1,0:T(8,128)(2,1)S(1)}, u32[]{:S(2)}, u32[]{:S(2)}) collective-permute-start(bf16[64,256]{1,0:T(8,128)(2,1)S(1)} %get-tuple-element.90), channel_id=1, source_target_pairs={{0,8},{4,12},{8,0},{12,4},{16,24},{20,28},{24,16},{28,20},{1,9},{5... | collective-permute-start | bytes 98312 | tf_op jit(solution)/shard_map/ppermute | solution.py:584
  72.5 6.9 %collective-permute-start.5 = (bf16[64,1024]{1,0:T(8,128)(2,1)S(1)}, bf16[64,1024]{1,0:T(8,128)(2,1)S(1)}, u32[]{:S(2)}, u32[]{:S(2)}) collective-permute-start(bf16[64,1024]{1,0:T(8,128)(2,1)S(1)} %shard_map.122.refs_0_), channel_id=1, source_target_pairs={{0,8},{4,12},{8,0},{12,4},{16,24},{20,28},{24,16},{28,20},{1,9},{5... | collective-permute-start | bytes 393224 | tf_op jit(solution)/shard_map/ppermute | solution.py:584
  74.1 6.3 %collective-permute-start.26 = (bf16[64,256]{1,0:T(8,128)(2,1)S(1)}, bf16[64,256]{1,0:T(8,128)(2,1)S(1)}, u32[]{:S(2)}, u32[]{:S(2)}) collective-permute-start(bf16[64,256]{1,0:T(8,128)(2,1)S(1)} %get-tuple-element.87), channel_id=1, source_target_pairs={{0,1},{1,0},{2,3},{3,2},{4,5},{5,4},{6,7},{7,6},{8,9},{9,8},{10,11... | collective-permute-start | bytes 98312 | tf_op jit(solution)/shard_map/ppermute | solution.py:578
  77.4 5.8 %collective-permute-start.31 = (bf16[64,256]{1,0:T(8,128)(2,1)S(1)}, bf16[64,256]{1,0:T(8,128)(2,1)S(1)}, u32[]{:S(2)}, u32[]{:S(2)}) collective-permute-start(bf16[64,256]{1,0:T(8,128)(2,1)S(1)} %shard_map.131), channel_id=1, source_target_pairs={{0,3},{1,2},{2,1},{3,0},{4,7},{5,6},{6,5},{7,4},{8,11},{9,10},{10,... | collective-permute-start | bytes 98312 | tf_op jit(solution)/shard_map/ppermute | solution.py:578
  85.7 11.8 %collective-permute-start.17 = (bf16[64,2048]{1,0:T(8,128)(2,1)S(1)}, bf16[64,2048]{1,0:T(8,128)(2,1)S(1)}, u32[]{:S(2)}, u32[]{:S(2)}) collective-permute-start(bf16[64,2048]{1,0:T(8,128)(2,1)S(1)} %get-tuple-element.60), channel_id=1, source_target_pairs={{0,8},{4,12},{8,0},{12,4},{16,24},{20,28},{24,16},{28,20},{1,9},{5... | collective-permute-start | bytes 786440 | tf_op jit(solution)/shard_map/ppermute | solution.py:584
  86.3 11.2 %collective-permute-start.18 = (bf16[64,2048]{1,0:T(8,128)(2,1)S(1)}, bf16[64,2048]{1,0:T(8,128)(2,1)S(1)}, u32[]{:S(2)}, u32[]{:S(2)}) collective-permute-start(bf16[64,2048]{1,0:T(8,128)(2,1)S(1)} %get-tuple-element.61), channel_id=1, source_target_pairs={{0,16},{4,20},{8,24},{12,28},{16,0},{20,4},{24,8},{28,12},{1,17},{... | collective-permute-start | bytes 786440 | tf_op jit(solution)/shard_map/ppermute | solution.py:584
  87.5 8.4 %collective-permute-start.35 = (f32[8,128]{1,0:T(8,128)S(1)}, f32[8,128]{1,0:T(8,128)S(1)}, u32[]{:S(2)}, u32[]{:S(2)}) collective-permute-start(f32[8,128]{1,0:T(8,128)S(1)} %shard_map.134.refs_0_), channel_id=1, source_target_pairs={{0,24},{4,28},{8,16},{12,20},{16,8},{20,12},{24,0},{28,4},{1,25},{... | collective-permute-start | bytes 12296 | tf_op jit(solution)/shard_map/ppermute | solution.py:584
  89.3 7.6 %collective-permute-start.34 = (f32[8,128]{1,0:T(8,128)S(1)}, f32[8,128]{1,0:T(8,128)S(1)}, u32[]{:S(2)}, u32[]{:S(2)}) collective-permute-start(f32[8,128]{1,0:T(8,128)S(1)} %shard_map.134.refs_0_), channel_id=1, source_target_pairs={{0,16},{4,20},{8,24},{12,28},{16,0},{20,4},{24,8},{28,12},{1,17},{... | collective-permute-start | bytes 12296 | tf_op jit(solution)/shard_map/ppermute | solution.py:584
  90.5 6.5 %collective-permute-start.33 = (f32[8,128]{1,0:T(8,128)S(1)}, f32[8,128]{1,0:T(8,128)S(1)}, u32[]{:S(2)}, u32[]{:S(2)}) collective-permute-start(f32[8,128]{1,0:T(8,128)S(1)} %shard_map.134.refs_0_), channel_id=1, source_target_pairs={{0,8},{4,12},{8,0},{12,4},{16,24},{20,28},{24,16},{28,20},{1,9},{5... | collective-permute-start | bytes 12296 | tf_op jit(solution)/shard_map/ppermute | solution.py:584
  95.8 8.1 %collective-permute-start.19 = (bf16[64,2048]{1,0:T(8,128)(2,1)S(1)}, bf16[64,2048]{1,0:T(8,128)(2,1)S(1)}, u32[]{:S(2)}, u32[]{:S(2)}) collective-permute-start(bf16[64,2048]{1,0:T(8,128)(2,1)S(1)} %get-tuple-element.62), channel_id=1, source_target_pairs={{0,24},{4,28},{8,16},{12,20},{16,8},{20,12},{24,0},{28,4},{1,25},{... | collective-permute-start | bytes 786440 | tf_op jit(solution)/shard_map/ppermute | solution.py:584
  (11 other events, 100.2 us)
where the time goes:
time: 105 us
  waiting for transfers between devices  48.8 us (46%)
  starting transfers between devices  38.2 us (36%)
  Pallas kernels  14.8 us (14%)
  local copies, waits for them, and re-layouts  1.38 us (1%)
  other arithmetic  1.06 us (1%)
    ppermute x18, waiting for transfers between devices, cross(): lax.ppermute(array, plane, [(p, p ^ cores * s) for p in range(members)])  24.6 us
    ppermute x18, starting transfers between devices, cross(): lax.ppermute(array, plane, [(p, p ^ cores * s) for p in range(members)])  22 us
    ppermute x10, waiting for transfers between devices, turn(): return lax.ppermute(array, 'tp', pairs)  21.5 us
    pallas_call x17, Pallas kernels, call(): pl.pallas_call(body, in_specs=specs, out_specs=[VMEM] * len(outs), out_sh...  14.8 us
    ppermute x10, starting transfers between devices, turn(): return lax.ppermute(array, 'tp', pairs)  13.8 us
    ppermute x1, waiting for transfers between devices, per_device(): lax.ppermute(joined[1] if d < ranks - 1 else joined[0], 'ctx', [(p, p - c...  2.69 us
  transfers between devices with their start and end apart: 36, of which 15 were waited for; matrix products, arithmetic and copies ran while one was open for 0% of the time, Pallas kernels for 7%

commit v1 on v0

--- a/solution.py
+++ b/solution.py
@@ -44,7 +44,7 @@
 
 
 def softplus(x):
-    return jnp.maximum(x, 0.0) + jnp.log(1.0 + jnp.exp(-jnp.abs(x)))
+    return jnp.maximum(x, 0.0) + jnp.log1p(jnp.exp(-jnp.abs(x)))
 
 
 def sigmoid(x):
@@ -241,14 +241,12 @@
         outs[m][...] = dv_ref[pl.ds(at, block), :].astype(bf16)
 
 
-def kernel_pre(
+def kernel_early(
     gates_ref,
     params_ref,
     tokens_ref,
     s_ref,
     u_ref,
-    z_ref,
-    end_ref,
     ut_ref,
     fade_ref,
     sink_ref,
@@ -258,12 +256,10 @@
     qn_ref,
     kn_ref,
     dq_ref,
-    dk_ref,
-    kend_ref,
     side_ref,
 ):
     q_ref, k_ref, g_ref = thirds(tokens_ref)
-    heads, n, hd = z_ref.shape
+    heads, n, hd = qn_ref.shape
     i, j = positions(n)
     rows, sums, sum_rows, strengths = shared(gates_ref, params_ref, heads, i, j)
     sides = []
@@ -277,7 +273,6 @@
         grown = jnp.exp(sums[h])
         fade = jnp.where(i <= j, jnp.exp(jnp.where(i <= j, sum_rows[h] - sums[h], 0.0)), 0.0)
         state = s_ref[h]
-        end = end_ref[h]
         ut_ref[h] = u_ref[h].T.astype(bf16)
         fade_ref[h] = fade
         sink_ref[h] = jnp.where(i < j, -fade * rows[h][1], 0.0)
@@ -287,20 +282,35 @@
         qn_ref[h] = q.astype(bf16)
         kn_ref[h] = k.astype(bf16)
         dq_in = grown * mm(g_ref[:, h * hd : (h + 1) * hd], state, 1, 1)
-        dk_in = -grown * mm(strengths[h] * z_ref[h], state, 1, 1)
         dq_ref[h] = dq_in
+        sides += [
+            jnp.sum(q * dq_in, axis=1, keepdims=True),
+            tail,
+            strengths[h],
+            grown,
+            jnp.broadcast_to(jnp.exp(last), (n, 1)),
+        ]
+    side_ref[...] = jnp.concatenate(sides, axis=1)
+
+
+def kernel_late(s_ref, kn_ref, side_ref, z_ref, end_ref, dk_ref, kend_ref, base_ref):
+    heads, _, _ = z_ref.shape
+    side = side_ref[...]
+    bases = []
+    for h in range(heads):
+        inner, tail, strength, grown, all_decay = [
+            side[:, 5 * h + index : 5 * h + index + 1] for index in range(5)
+        ]
+        state = s_ref[h]
+        end = end_ref[h]
+        k = kn_ref[h]
+        dk_in = -grown * mm(strength * z_ref[h], state, 1, 1)
         dk_ref[h] = dk_in
         kend_ref[h] = tail * mm(k, end)
-        sides.append(
-            jnp.sum(q * dq_in, axis=1, keepdims=True) + jnp.sum(k * dk_in, axis=1, keepdims=True)
-        )
-        sides.append(tail)
-        sides.append(strengths[h])
-        total = jnp.exp(last) * jnp.sum(
-            jnp.sum(state * end, axis=1, keepdims=True), axis=0, keepdims=True
-        )
-        sides.append(jnp.broadcast_to(total, (n, 1)))
-    side_ref[...] = jnp.concatenate(sides, axis=1)
+        bases.append(inner + jnp.sum(k.astype(f32) * dk_in, axis=1, keepdims=True))
+        total = jnp.sum(jnp.sum(state * end, axis=1, keepdims=True), axis=0, keepdims=True)
+        bases.append(all_decay * total)
+    base_ref[...] = jnp.concatenate(bases, axis=1)
 
 
 def kernel_gates(
@@ -316,6 +326,7 @@
     ks_ref,
     kend_ref,
     side_ref,
+    base_ref,
     *refs,
     steps,
 ):
@@ -331,11 +342,12 @@
     i, j = positions(n)
     rows = gate_rows(gates_ref, params_ref, heads)
     side = side_ref[...]
+    bases = base_ref[...]
     changes, products, sums, extra = [], [], [], []
     for h in range(heads):
         cols = slice(h * hd, (h + 1) * hd)
-        base = side[:, 4 * h : 4 * h + 1]
-        strength = side[:, 4 * h + 2 : 4 * h + 3]
+        base = bases[:, 2 * h : 2 * h + 1]
+        strength = side[:, 5 * h + 2 : 5 * h + 3]
         z = z_ref[h]
         new = mm(ut_ref[h], strength * (v_ref[:, cols] - ks_ref[h]))
         near = fade_ref[h] * mm(new, g_ref[:, cols], 1, 1)
@@ -348,7 +360,7 @@
         changes.append(base - jnp.sum(pairs, axis=1, keepdims=True) - weight)
         products.append(jnp.sum(z * new, axis=1, keepdims=True))
         sums.append(jnp.sum(pairs, axis=0, keepdims=True))
-        extra.append(jnp.sum(weight, axis=0, keepdims=True) + side[0:1, 4 * h + 3 : 4 * h + 4])
+        extra.append(jnp.sum(weight, axis=0, keepdims=True) + bases[0:1, 2 * h + 1 : 2 * h + 2])
     from_rows = to_columns(sums)
     strength_rows = to_rows(products)
     si = lax.broadcasted_iota(jnp.int32, small_ref.shape, 0)
@@ -378,7 +390,7 @@
         cols = slice(h * hd, (h + 1) * hd)
         qraw, qinv = units(q_ref, h, hd)
         kraw, kinv = units(k_ref, h, hd)
-        tail = side[:, 4 * h + 1 : 4 * h + 2]
+        tail = side[:, 5 * h + 1 : 5 * h + 2]
         both = both_ref[h]
         by_key = mm(both, kn_ref[h], 0, 0)
         dq = by_key[:n] + dq_in_ref[h]
@@ -467,16 +479,16 @@
 
 
 def kernel_input(*refs, chips, group, first, final):
-    grads = refs[:chips]
+    grads, refs = refs[:2], refs[2:]
     chunks = pieces(group)
-    mine = list(refs[chips : chips + chunks])
-    theirs = list(refs[chips + chunks : chips + 2 * chunks])
-    rest = list(refs[chips + 2 * chunks :])
+    mine = list(refs[:chunks])
+    theirs = list(refs[chunks : 2 * chunks])
+    rest = list(refs[2 * chunks :])
     before = None if first else rest.pop(0)
     scratch = rest.pop()
     core = place_core()
     level = place_level()
-    block = grads[0].shape[0]
+    block = 2 * grads[0].shape[0] // chips
     part, width = mine[0].shape
     rows = jnp.concatenate([ref[...] for ref in grads], axis=0)
     for index, (found, at) in enumerate(((mine, core * part), (theirs, (1 - core) * part))):
@@ -497,13 +509,22 @@
             rest[0][index] = total
 
 
-def kernel_assemble(*refs):
-    out_ref = refs[-1]
-    width = refs[0].shape[1]
+def kernel_assemble(*refs, chips):
+    small, parts = refs[:chips], refs[chips : 2 * chips]
+    out_ref, decay_ref = refs[2 * chips :]
+    width = parts[0].shape[1]
     me = place_chip()
-    for s, ref in enumerate(refs[:-1]):
+    for s, ref in enumerate(parts):
         at = pl.multiple_of((me ^ s) * width, width)
         out_ref[:, pl.ds(at, width)] = ref[...]
+    total = functools.reduce(jnp.add, [ref[...] for ref in small])
+    decay_ref[...] = total[: decay_ref.shape[0], : decay_ref.shape[1]]
+
+
+def kernel_stack(first_ref, second_ref, out_ref):
+    n = first_ref.shape[0]
+    out_ref[:n, :] = first_ref[...]
+    out_ref[n:, :] = second_ref[...]
 
 
 def kernel_join(*refs):
@@ -527,17 +548,10 @@
 HBM = pl.BlockSpec(memory_space=pltpu.HBM)
 
 
-def call(body, args, specs, outs, scratch=(), loads=()):
-    specs = list(specs)
-    grid = {}
-    if loads:
-        grid = dict(grid=(1,))
-        for index in loads:
-            shape = args[index].shape
-            specs[index] = pl.BlockSpec(shape, lambda i, rank=len(shape): (0,) * rank)
+def call(body, args, specs, outs, scratch=()):
     return pl.pallas_call(
         body,
-        in_specs=specs,
+        in_specs=list(specs),
         out_specs=[VMEM] * len(outs),
         out_shape=list(outs),
         scratch_shapes=list(scratch),
@@ -545,7 +559,6 @@
             flops=3 * 10**9, bytes_accessed=20 * 10**6, transcendentals=0
         ),
         compiler_params=pltpu.CompilerParams(vmem_limit_bytes=12 * 1024 * 1024),
-        **grid,
     )(*args)
 
 
@@ -649,7 +662,17 @@
     dv_row = call(
         kernel_join, tuple(dv_cols), (VMEM,) * steps, (struct((block, steps * width), bf16),)
     )[0]
-    dv_parts = [dv_row if s == 0 else cross(dv_row, s) for s in range(chips)]
+    dv_parts = [dv_row]
+    for e in range((chips - 1).bit_length()):
+        if e:
+            dv_row = call(
+                kernel_stack,
+                tuple(dv_parts),
+                (VMEM,) * 2,
+                (struct((2 * dv_row.shape[0], dv_row.shape[1]), bf16),),
+            )[0]
+        dv_parts = [dv_row, cross(dv_row, 2**e)]
+
 
     groups = [tuple(range(steps - 1)), (steps - 1,)]
     v_blocks = []
@@ -693,10 +716,10 @@
     square = struct((heads, length, length), f32)
     tall = struct((heads, length, hd), f32)
     tall_half = struct((heads, length, hd), bf16)
-    ut, fade, sink, gram, cross_prod, k_state, qn, kn, dq_in, dk_in, k_end, side = call(
-        kernel_pre,
-        (gates, decay_params, stacked, states, inverse, z, end),
-        (VMEM,) * 7,
+    ut, fade, sink, gram, cross_prod, k_state, qn, kn, dq_in, side = call(
+        kernel_early,
+        (gates, decay_params, stacked, states, inverse),
+        (VMEM,) * 5,
         (
             struct((heads, length, length), bf16),
             square,
@@ -707,10 +730,14 @@
             tall_half,
             tall_half,
             tall,
-            tall,
-            tall,
-            struct((length, 4 * heads), f32),
+            struct((length, 5 * heads), f32),
         ),
+    )
+    dk_in, k_end, base = call(
+        kernel_late,
+        (states, kn, side, z, end),
+        (VMEM,) * 5,
+        (tall, tall, struct((length, 2 * heads), f32)),
     )
     gate, small, both, new = call(
         functools.partial(kernel_gates, steps=steps),
@@ -727,9 +754,10 @@
             k_state,
             k_end,
             side,
+            base,
             *v_blocks,
         ),
-        (VMEM,) * (12 + steps),
+        (VMEM,) * (13 + steps),
         (
             struct((2, heads, length), f32),
             struct((8, 128), f32),
@@ -746,11 +774,13 @@
     )
     tile = (struct(small.shape, f32),)
     small = call(kernel_decay, (small, swap(small)), (VMEM, VMEM), tile)[0]
-    input_grad = call(
-        kernel_assemble, tuple(in_back), (VMEM,) * chips, (struct((block, model), bf16),)
-    )[0]
     shares = [small if s == 0 else cross(small, s) for s in range(chips)]
-    decay_grad = call(kernel_decay, tuple(shares), (VMEM,) * chips, (struct((2, heads), f32),))[0]
+    input_grad, decay_grad = call(
+        functools.partial(kernel_assemble, chips=chips),
+        (*shares, *in_back),
+        (VMEM,) * (2 * chips),
+        (struct((block, model), bf16), struct((2, heads), f32)),
+    )
     return (input_grad[None], dq[None], dk[None], gate[:, None], decay_grad)
 
 

time: 105 us -> 103 us (0.981)
  starting transfers between devices: 38.2 us -> 32.9 us
  waiting for transfers between devices: 48.8 us -> 51.8 us
    ppermute x10, waiting for transfers between devices: 21.5 us -> 27.1 us  [turn(): return lax.ppermute(array, 'tp', pairs)]
    ppermute x10, starting transfers between devices: 13.8 us -> 9.91 us  [turn(): return lax.ppermute(array, 'tp', pairs)]
    ppermute x18 -> x17, waiting for transfers between devices: 24.6 us -> 21.8 us  [cross(): lax.ppermute(array, plane, [(p, p ^ cores * s) for p in range(members)])]
    ppermute x18 -> x17, starting transfers between devices: 22 us -> 20.5 us  [cross(): lax.ppermute(array, plane, [(p, p ^ cores * s) for p in range(members)])]
    pallas_call x17 -> x18, Pallas kernels: 14.8 us -> 14.4 us  [call(): pl.pallas_call(body, in_specs=list(specs), out_specs=[VMEM] * len(outs),...]
  transfers between devices with their start and end apart: 36 -> 35, of which waited for: 15 -> 12; matrix products, arithmetic and copies ran while one was open for 0% -> 0% of each run, Pallas kernels for 7% -> 9%
where the time goes in v1:
time: 103 us; the launch traced here: 102 us
  waiting for transfers between devices  51.8 us (50%)
  starting transfers between devices  32.9 us (32%)
  Pallas kernels  14.4 us (14%)
  local copies, waits for them, and re-layouts  1.38 us (1%)
  other arithmetic  1.06 us (1%)
    ppermute x10, waiting for transfers between devices, turn(): return lax.ppermute(array, 'tp', pairs)  27.1 us
    ppermute x17, waiting for transfers between devices, cross(): lax.ppermute(array, plane, [(p, p ^ cores * s) for p in range(members)])  21.8 us
    ppermute x17, starting transfers between devices, cross(): lax.ppermute(array, plane, [(p, p ^ cores * s) for p in range(members)])  20.5 us
    pallas_call x18, Pallas kernels, call(): pl.pallas_call(body, in_specs=list(specs), out_specs=[VMEM] * len(outs),...  14.4 us
    ppermute x10, starting transfers between devices, turn(): return lax.ppermute(array, 'tp', pairs)  9.91 us
    ppermute x1, waiting for transfers between devices, per_device(): lax.ppermute(joined[1] if d < ranks - 1 else joined[0], 'ctx', [(p, p - c...  2.69 us
  transfers between devices with their start and end apart: 35, of which 12 were waited for; matrix products, arithmetic and copies ran while one was open for 0% of the time, Pallas kernels for 9%

profile of v1, /device:TPU:0, one launch (start us, length us, event | category | flops | bytes accessed | tf_op | source)
XLA Modules:
  0.0 102.4 jit_solution(16276264514967474889)
XLA Ops:
  0.6 1.1 %pad_maximum_fusion.tokens_ref = bf16[768,256]{1,0:T(8,128)(2,1)S(1)} fusion(bf16[256,256]{1,0:T(8,128)(2,1)} %bitcast.19, bf16[256,256]{1,0:T(8,128)(2,1)} %bitcast.20, bf16[256,256]{1,0:T(8,128)(2,1)} %bitcast.21), kind=kLoop, calls=%fused_computation | loop fusion | flops 1179648 | bytes 786432 | tf_op jit(solution)/shard_map/concatenate | solution.py:586
  3.1 4.3 %shard_map.119 = (bf16[2,128,256]{2,1,0:T(8,128)(2,1)S(1)}, bf16[2,256,128]{2,1,0:T(8,128)(2,1)S(1)}, f32[2,256,128]{2,1,0:T(8,128)S(1)}, f32[2,256,256]{2,1,0:T(8,128)S(1)}) custom-call(f32[2,2,256]{2,1,0:T(2,128)S(1)} %bitcast.15, f32[2,2]{1,0:T(2,128)S(1)} %copy-done.5, bf16[768,256]{1,0:T(8,128)(2,1)S(1)} %pad_maximum_fusion.tokens_ref), custom_call_target="tpu_custom_call" | custom-call | flops 3000000000 | bytes 20000000 | tf_op jit(solution)/shard_map/pallas_call | solution.py:552
  8.0 3.7 %collective-permute-start.6 = (bf16[1024,256]{1,0:T(8,128)(2,1)S(1)}, bf16[1024,256]{1,0:T(8,128)(2,1)S(1)}, u32[]{:S(2)}, u32[]{:S(2)}) collective-permute-start(bf16[1024,256]{1,0:T(8,128)(2,1)S(1)} %copy-done.1), channel_id=1, source_target_pairs={{0,2},{1,3},{2,0},{3,1},{4,6},{5,7},{6,4},{7,5},{8,10},{9,11},{10,... | collective-permute-start | bytes 1572872 | tf_op jit(solution)/shard_map/ppermute | solution.py:591
  11.6 1.6 %collective-permute-start.5 = (bf16[1024,256]{1,0:T(8,128)(2,1)S(1)}, bf16[1024,256]{1,0:T(8,128)(2,1)S(1)}, u32[]{:S(2)}, u32[]{:S(2)}) collective-permute-start(bf16[1024,256]{1,0:T(8,128)(2,1)S(1)} %copy-done.1), channel_id=1, source_target_pairs={{0,1},{1,0},{2,3},{3,2},{4,5},{5,4},{6,7},{7,6},{8,9},{9,8},{10,11... | collective-permute-start | bytes 1572872 | tf_op jit(solution)/shard_map/ppermute | solution.py:591
  13.4 1.3 %collective-permute-start.1 = (bf16[2,128,128]{2,1,0:T(8,128)(2,1)S(1)}, bf16[2,128,128]{2,1,0:T(8,128)(2,1)S(1)}, u32[]{:S(2)}, u32[]{:S(2)}) collective-permute-start(bf16[2,128,128]{2,1,0:T(8,128)(2,1)S(1)} %shard_map.120), channel_id=1, source_target_pairs={{8,0},{12,4},{9,1},{13,5},{10,2},{14,6},{11,3},{15,7},{24,16},{28,... | collective-permute-start | bytes 196616 | tf_op jit(solution)/shard_map/ppermute | solution.py:636
  14.8 2.7 %collective-permute-start.2 = (bf16[64,2048]{1,0:T(8,128)(2,1)S(1)}, bf16[64,2048]{1,0:T(8,128)(2,1)S(1)}, u32[]{:S(2)}, u32[]{:S(2)}) collective-permute-start(bf16[64,2048]{1,0:T(8,128)(2,1)S(1)} %get-tuple-element.72), channel_id=1, source_target_pairs={{0,8},{4,12},{8,0},{12,4},{16,24},{20,28},{24,16},{28,20},{1,9},{5... | collective-permute-start | bytes 786440 | tf_op jit(solution)/shard_map/ppermute | solution.py:597
  17.5 2.7 %collective-permute-done.1.refs_0_ = bf16[2,128,128]{2,1,0:T(8,128)(2,1)S(1)} collective-permute-done((bf16[2,128,128]{2,1,0:T(8,128)(2,1)S(1)}, bf16[2,128,128]{2,1,0:T(8,128)(2,1)S(1)}, u32[]{:S(2)}, u32[]{:S(2)}) %collective-permute-start.1) | collective-permute-done | bytes 65568 | tf_op jit(solution)/shard_map/ppermute | solution.py:636
  21.9 15.1 %collective-permute-done.27.refs_1_ = bf16[64,256]{1,0:T(8,128)(2,1)S(1)} collective-permute-done((bf16[64,256]{1,0:T(8,128)(2,1)S(1)}, bf16[64,256]{1,0:T(8,128)(2,1)S(1)}, u32[]{:S(2)}, u32[]{:S(2)}) %collective-permute-start.27) | collective-permute-done | bytes 32800 | tf_op jit(solution)/shard_map/ppermute | solution.py:591
  37.8 5.1 %collective-permute-done.29.refs_3_ = bf16[64,256]{1,0:T(8,128)(2,1)S(1)} collective-permute-done((bf16[64,256]{1,0:T(8,128)(2,1)S(1)}, bf16[64,256]{1,0:T(8,128)(2,1)S(1)}, u32[]{:S(2)}, u32[]{:S(2)}) %collective-permute-start.29) | collective-permute-done | bytes 32800 | tf_op jit(solution)/shard_map/ppermute | solution.py:591
  42.9 1.5 %collective-permute-start.3 = (bf16[64,2048]{1,0:T(8,128)(2,1)S(1)}, bf16[64,2048]{1,0:T(8,128)(2,1)S(1)}, u32[]{:S(2)}, u32[]{:S(2)}) collective-permute-start(bf16[64,2048]{1,0:T(8,128)(2,1)S(1)} %get-tuple-element.73), channel_id=1, source_target_pairs={{0,16},{4,20},{8,24},{12,28},{16,0},{20,4},{24,8},{28,12},{1,17},{... | collective-permute-start | bytes 786440 | tf_op jit(solution)/shard_map/ppermute | solution.py:597
  44.4 1.5 %collective-permute-start.4 = (bf16[64,2048]{1,0:T(8,128)(2,1)S(1)}, bf16[64,2048]{1,0:T(8,128)(2,1)S(1)}, u32[]{:S(2)}, u32[]{:S(2)}) collective-permute-start(bf16[64,2048]{1,0:T(8,128)(2,1)S(1)} %get-tuple-element.74), channel_id=1, source_target_pairs={{0,24},{4,28},{8,16},{12,20},{16,8},{20,12},{24,0},{28,4},{1,25},{... | collective-permute-start | bytes 786440 | tf_op jit(solution)/shard_map/ppermute | solution.py:597
  45.9 1.3 %collective-permute-start.16 = (bf16[1024,256]{1,0:T(8,128)(2,1)S(1)}, bf16[1024,256]{1,0:T(8,128)(2,1)S(1)}, u32[]{:S(2)}, u32[]{:S(2)}) collective-permute-start(bf16[1024,256]{1,0:T(8,128)(2,1)S(1)} %collective-permute-done.6.refs_6_.refs_4_), channel_id=1, source_target_pairs={{1,0},{2,3},{5,4},{6,7},{9,8},{10,11},{13,12},{14,15},{17,16},{18,... | collective-permute-start | bytes 1572872 | tf_op jit(solution)/shard_map/ppermute | solution.py:591
  48.2 3.7 %collective-permute-done.3.refs_2_ = bf16[64,2048]{1,0:T(8,128)(2,1)S(1)} collective-permute-done((bf16[64,2048]{1,0:T(8,128)(2,1)S(1)}, bf16[64,2048]{1,0:T(8,128)(2,1)S(1)}, u32[]{:S(2)}, u32[]{:S(2)}) %collective-permute-start.3) | collective-permute-done | bytes 262176 | tf_op jit(solution)/shard_map/ppermute | solution.py:597
  52.0 3.8 %collective-permute-done.4.refs_3_ = bf16[64,2048]{1,0:T(8,128)(2,1)S(1)} collective-permute-done((bf16[64,2048]{1,0:T(8,128)(2,1)S(1)}, bf16[64,2048]{1,0:T(8,128)(2,1)S(1)}, u32[]{:S(2)}, u32[]{:S(2)}) %collective-permute-start.4) | collective-permute-done | bytes 262176 | tf_op jit(solution)/shard_map/ppermute | solution.py:597
  57.0 2.1 %collective-permute-done.16.refs_5_.refs_3_ = bf16[1024,256]{1,0:T(8,128)(2,1)S(1)} collective-permute-done((bf16[1024,256]{1,0:T(8,128)(2,1)S(1)}, bf16[1024,256]{1,0:T(8,128)(2,1)S(1)}, u32[]{:S(2)}, u32[]{:S(2)}) %collective-permute-start.16) | collective-permute-done | bytes 524320 | tf_op jit(solution)/shard_map/ppermute | solution.py:591
  60.7 1.6 %collective-permute-start.10 = (bf16[64,768]{1,0:T(8,128)(2,1)S(1)}, bf16[64,768]{1,0:T(8,128)(2,1)S(1)}, u32[]{:S(2)}, u32[]{:S(2)}) collective-permute-start(bf16[64,768]{1,0:T(8,128)(2,1)S(1)} %get-tuple-element.76), channel_id=1, source_target_pairs={{0,8},{4,12},{8,0},{12,4},{16,24},{20,28},{24,16},{28,20},{1,9},{5... | collective-permute-start | bytes 294920 | tf_op jit(solution)/shard_map/ppermute | solution.py:597
  62.3 1.5 %collective-permute-start.11 = (bf16[64,768]{1,0:T(8,128)(2,1)S(1)}, bf16[64,768]{1,0:T(8,128)(2,1)S(1)}, u32[]{:S(2)}, u32[]{:S(2)}) collective-permute-start(bf16[64,768]{1,0:T(8,128)(2,1)S(1)} %get-tuple-element.77), channel_id=1, source_target_pairs={{0,16},{4,20},{8,24},{12,28},{16,0},{20,4},{24,8},{28,12},{1,17},{... | collective-permute-start | bytes 294920 | tf_op jit(solution)/shard_map/ppermute | solution.py:597
  64.9 1.6 %collective-permute-start.19 = (bf16[64,256]{1,0:T(8,128)(2,1)S(1)}, bf16[64,256]{1,0:T(8,128)(2,1)S(1)}, u32[]{:S(2)}, u32[]{:S(2)}) collective-permute-start(bf16[64,256]{1,0:T(8,128)(2,1)S(1)} %get-tuple-element.83), channel_id=1, source_target_pairs={{0,8},{4,12},{8,0},{12,4},{16,24},{20,28},{24,16},{28,20},{1,9},{5... | collective-permute-start | bytes 98312 | tf_op jit(solution)/shard_map/ppermute | solution.py:597
  66.5 3.2 %collective-permute-done.10.refs_1_ = bf16[64,768]{1,0:T(8,128)(2,1)S(1)} collective-permute-done((bf16[64,768]{1,0:T(8,128)(2,1)S(1)}, bf16[64,768]{1,0:T(8,128)(2,1)S(1)}, u32[]{:S(2)}, u32[]{:S(2)}) %collective-permute-start.10) | collective-permute-done | bytes 98336 | tf_op jit(solution)/shard_map/ppermute | solution.py:597
  69.6 1.5 %collective-permute-start.20 = (bf16[64,256]{1,0:T(8,128)(2,1)S(1)}, bf16[64,256]{1,0:T(8,128)(2,1)S(1)}, u32[]{:S(2)}, u32[]{:S(2)}) collective-permute-start(bf16[64,256]{1,0:T(8,128)(2,1)S(1)} %get-tuple-element.84), channel_id=1, source_target_pairs={{0,16},{4,20},{8,24},{12,28},{16,0},{20,4},{24,8},{28,12},{1,17},{... | collective-permute-start | bytes 98312 | tf_op jit(solution)/shard_map/ppermute | solution.py:597
  72.2 1.3 %collective-permute-done.20.refs_2_ = bf16[64,256]{1,0:T(8,128)(2,1)S(1)} collective-permute-done((bf16[64,256]{1,0:T(8,128)(2,1)S(1)}, bf16[64,256]{1,0:T(8,128)(2,1)S(1)}, u32[]{:S(2)}, u32[]{:S(2)}) %collective-permute-start.20) | collective-permute-done | bytes 32800 | tf_op jit(solution)/shard_map/ppermute | solution.py:597
  73.6 2.4 %collective-permute-done.21.refs_3_ = bf16[64,256]{1,0:T(8,128)(2,1)S(1)} collective-permute-done((bf16[64,256]{1,0:T(8,128)(2,1)S(1)}, bf16[64,256]{1,0:T(8,128)(2,1)S(1)}, u32[]{:S(2)}, u32[]{:S(2)}) %collective-permute-start.21) | collective-permute-done | bytes 32800 | tf_op jit(solution)/shard_map/ppermute | solution.py:597
  77.0 4.8 %collective-permute-done.22.refs_3_ = bf16[64,256]{1,0:T(8,128)(2,1)S(1)} collective-permute-done((bf16[64,256]{1,0:T(8,128)(2,1)S(1)}, bf16[64,256]{1,0:T(8,128)(2,1)S(1)}, u32[]{:S(2)}, u32[]{:S(2)}) %collective-permute-start.22) | collective-permute-done | bytes 32800 | tf_op jit(solution)/shard_map/ppermute | solution.py:591
  81.8 1.7 %shard_map.129 = (f32[2,2,256]{2,1,0:T(2,128)}, f32[8,128]{1,0:T(8,128)S(1)}, bf16[2,256,512]{2,1,0:T(8,128)(2,1)S(1)}, bf16[2,256,128]{2,1,0:T(8,128)(2,1)S(1)}) custom-call(f32[2,2,256]{2,1,0:T(2,128)S(1)} %bitcast.18, f32[2,2]{1,0:T(2,128)S(1)} %copy-done.6, bf16[768,256]{1,0:T(8,128)(2,1)S(1)} %pad_maximum_fusion.tokens_ref, ...), custom_call_target="tpu_custom_call" | custom-call | flops 3000000000 | bytes 20000000 | tf_op jit(solution)/shard_map/pallas_call | solution.py:552
  83.5 1.0 shard_map.133.refs_6_
  84.7 1.6 %collective-permute-start.26 = (f32[8,128]{1,0:T(8,128)S(1)}, f32[8,128]{1,0:T(8,128)S(1)}, u32[]{:S(2)}, u32[]{:S(2)}) collective-permute-start(f32[8,128]{1,0:T(8,128)S(1)} %shard_map.130.refs_0_), channel_id=1, source_target_pairs={{0,24},{4,28},{8,16},{12,20},{16,8},{20,12},{24,0},{28,4},{1,25},{... | collective-permute-start | bytes 12296 | tf_op jit(solution)/shard_map/ppermute | solution.py:597
  87.5 1.5 %collective-permute-start.33 = (bf16[64,2048]{1,0:T(8,128)(2,1)S(1)}, bf16[64,2048]{1,0:T(8,128)(2,1)S(1)}, u32[]{:S(2)}, u32[]{:S(2)}) collective-permute-start(bf16[64,2048]{1,0:T(8,128)(2,1)S(1)} %get-tuple-element.93), channel_id=1, source_target_pairs={{0,16},{4,20},{8,24},{12,28},{16,0},{20,4},{24,8},{28,12},{1,17},{... | collective-permute-start | bytes 786440 | tf_op jit(solution)/shard_map/ppermute | solution.py:597
  89.1 1.6 %collective-permute-start.34 = (bf16[64,2048]{1,0:T(8,128)(2,1)S(1)}, bf16[64,2048]{1,0:T(8,128)(2,1)S(1)}, u32[]{:S(2)}, u32[]{:S(2)}) collective-permute-start(bf16[64,2048]{1,0:T(8,128)(2,1)S(1)} %get-tuple-element.94), channel_id=1, source_target_pairs={{0,24},{4,28},{8,16},{12,20},{16,8},{20,12},{24,0},{28,4},{1,25},{... | collective-permute-start | bytes 786440 | tf_op jit(solution)/shard_map/ppermute | solution.py:597
  91.2 1.4 %collective-permute-start.24 = (f32[8,128]{1,0:T(8,128)S(1)}, f32[8,128]{1,0:T(8,128)S(1)}, u32[]{:S(2)}, u32[]{:S(2)}) collective-permute-start(f32[8,128]{1,0:T(8,128)S(1)} %shard_map.130.refs_0_), channel_id=1, source_target_pairs={{0,8},{4,12},{8,0},{12,4},{16,24},{20,28},{24,16},{28,20},{1,9},{5... | collective-permute-start | bytes 12296 | tf_op jit(solution)/shard_map/ppermute | solution.py:597
  92.5 1.4 %shard_map.136 = (bf16[256,256]{1,0:T(8,128)(2,1)}, bf16[256,256]{1,0:T(8,128)(2,1)}) custom-call(bf16[768,256]{1,0:T(8,128)(2,1)S(1)} %pad_maximum_fusion.tokens_ref, bf16[2,256,128]{2,1,0:T(8,128)(2,1)S(1)} %get-tuple-element.96.qn_ref, bf16[2,256,128]{2,1,0:T(8,128)(2,1)S(1)} %get-tuple-element.66.kn_ref, f32[2,128,128]{2,1,0:T(8,128)S(1)} %get-tuple-element.68.end_ref, ...), custom_call_target="tpu_custom_call" | custom-call | flops 3000000000 | bytes 20000000 | tf_op jit(solution)/shard_map/pallas_call | solution.py:552
  94.0 7.3 %collective-permute-done.25.refs_2_ = f32[8,128]{1,0:T(8,128)S(1)} collective-permute-done((f32[8,128]{1,0:T(8,128)S(1)}, f32[8,128]{1,0:T(8,128)S(1)}, u32[]{:S(2)}, u32[]{:S(2)}) %collective-permute-start.25) | collective-permute-done | bytes 4128 | tf_op jit(solution)/shard_map/ppermute | solution.py:597
  101.3 1.1 %shard_map.135 = (bf16[64,8192]{1,0:T(8,128)(2,1)}, f32[2,2]{1,0:T(2,128)}) custom-call(f32[8,128]{1,0:T(8,128)S(1)} %shard_map.130.refs_0_, f32[8,128]{1,0:T(8,128)S(1)} %collective-permute-done.24.refs_1_, f32[8,128]{1,0:T(8,128)S(1)} %collective-permute-done.25.refs_2_, f32[8,128]{1,0:T(8,128)S(1)} %collective-permute-done.26.refs_3_, ...), custom_call_target="tpu_custom_call" | custom-call | flops 3000000000 | bytes 20000000 | tf_op jit(solution)/shard_map/pallas_call | solution.py:552
  (71 shorter events, 13.4 us)
Async XLA Ops:
  7.4 5.8 %collective-permute-start = (bf16[2,128,256]{2,1,0:T(8,128)(2,1)S(1)}, bf16[2,128,256]{2,1,0:T(8,128)(2,1)S(1)}, u32[]{:S(2)}, u32[]{:S(2)}) collective-permute-start(bf16[2,128,256]{2,1,0:T(8,128)(2,1)S(1)} %get-tuple-element.57.bc_ref), channel_id=1, source_target_pairs={{0,4},{4,0},{8,12},{12,8},{16,20},{20,16},{24,28},{28,24},{1,5},{5... | collective-permute-start | bytes 393224 | tf_op jit(solution)/shard_map/ppermute | solution.py:594
  8.0 37.9 %collective-permute-start.6 = (bf16[1024,256]{1,0:T(8,128)(2,1)S(1)}, bf16[1024,256]{1,0:T(8,128)(2,1)S(1)}, u32[]{:S(2)}, u32[]{:S(2)}) collective-permute-start(bf16[1024,256]{1,0:T(8,128)(2,1)S(1)} %copy-done.1), channel_id=1, source_target_pairs={{0,2},{1,3},{2,0},{3,1},{4,6},{5,7},{6,4},{7,5},{8,10},{9,11},{10,... | collective-permute-start | bytes 1572872 | tf_op jit(solution)/shard_map/ppermute | solution.py:591
  11.6 44.1 %collective-permute-start.5 = (bf16[1024,256]{1,0:T(8,128)(2,1)S(1)}, bf16[1024,256]{1,0:T(8,128)(2,1)S(1)}, u32[]{:S(2)}, u32[]{:S(2)}) collective-permute-start(bf16[1024,256]{1,0:T(8,128)(2,1)S(1)} %copy-done.1), channel_id=1, source_target_pairs={{0,1},{1,0},{2,3},{3,2},{4,5},{5,4},{6,7},{7,6},{8,9},{9,8},{10,11... | collective-permute-start | bytes 1572872 | tf_op jit(solution)/shard_map/ppermute | solution.py:591
  13.4 6.9 %collective-permute-start.1 = (bf16[2,128,128]{2,1,0:T(8,128)(2,1)S(1)}, bf16[2,128,128]{2,1,0:T(8,128)(2,1)S(1)}, u32[]{:S(2)}, u32[]{:S(2)}) collective-permute-start(bf16[2,128,128]{2,1,0:T(8,128)(2,1)S(1)} %shard_map.120), channel_id=1, source_target_pairs={{8,0},{12,4},{9,1},{13,5},{10,2},{14,6},{11,3},{15,7},{24,16},{28,... | collective-permute-start | bytes 196616 | tf_op jit(solution)/shard_map/ppermute | solution.py:636
  14.8 29.6 %collective-permute-start.2 = (bf16[64,2048]{1,0:T(8,128)(2,1)S(1)}, bf16[64,2048]{1,0:T(8,128)(2,1)S(1)}, u32[]{:S(2)}, u32[]{:S(2)}) collective-permute-start(bf16[64,2048]{1,0:T(8,128)(2,1)S(1)} %get-tuple-element.72), channel_id=1, source_target_pairs={{0,8},{4,12},{8,0},{12,4},{16,24},{20,28},{24,16},{28,20},{1,9},{5... | collective-permute-start | bytes 786440 | tf_op jit(solution)/shard_map/ppermute | solution.py:597
  20.6 16.5 %collective-permute-start.27 = (bf16[64,256]{1,0:T(8,128)(2,1)S(1)}, bf16[64,256]{1,0:T(8,128)(2,1)S(1)}, u32[]{:S(2)}, u32[]{:S(2)}) collective-permute-start(bf16[64,256]{1,0:T(8,128)(2,1)S(1)} %get-tuple-element.88), channel_id=1, source_target_pairs={{0,1},{1,0},{2,3},{3,2},{4,5},{5,4},{6,7},{7,6},{8,9},{9,8},{10,11... | collective-permute-start | bytes 98312 | tf_op jit(solution)/shard_map/ppermute | solution.py:591
  21.1 16.0 %collective-permute-start.28 = (bf16[64,256]{1,0:T(8,128)(2,1)S(1)}, bf16[64,256]{1,0:T(8,128)(2,1)S(1)}, u32[]{:S(2)}, u32[]{:S(2)}) collective-permute-start(bf16[64,256]{1,0:T(8,128)(2,1)S(1)} %get-tuple-element.89), channel_id=1, source_target_pairs={{0,2},{1,3},{2,0},{3,1},{4,6},{5,7},{6,4},{7,5},{8,10},{9,11},{10,... | collective-permute-start | bytes 98312 | tf_op jit(solution)/shard_map/ppermute | solution.py:591
  37.1 5.8 %collective-permute-start.29 = (bf16[64,256]{1,0:T(8,128)(2,1)S(1)}, bf16[64,256]{1,0:T(8,128)(2,1)S(1)}, u32[]{:S(2)}, u32[]{:S(2)}) collective-permute-start(bf16[64,256]{1,0:T(8,128)(2,1)S(1)} %get-tuple-element.90), channel_id=1, source_target_pairs={{0,3},{1,2},{2,1},{3,0},{4,7},{5,6},{6,5},{7,4},{8,11},{9,10},{10,... | collective-permute-start | bytes 98312 | tf_op jit(solution)/shard_map/ppermute | solution.py:591
  37.1 19.8 %collective-permute-start.15 = (bf16[1024,256]{1,0:T(8,128)(2,1)S(1)}, bf16[1024,256]{1,0:T(8,128)(2,1)S(1)}, u32[]{:S(2)}, u32[]{:S(2)}) collective-permute-start(bf16[1024,256]{1,0:T(8,128)(2,1)S(1)} %copy-done.1), channel_id=1, source_target_pairs={{1,2},{2,1},{5,6},{6,5},{9,10},{10,9},{13,14},{14,13},{17,18},{18,... | collective-permute-start | bytes 1572872 | tf_op jit(solution)/shard_map/ppermute | solution.py:591
  42.9 9.1 %collective-permute-start.3 = (bf16[64,2048]{1,0:T(8,128)(2,1)S(1)}, bf16[64,2048]{1,0:T(8,128)(2,1)S(1)}, u32[]{:S(2)}, u32[]{:S(2)}) collective-permute-start(bf16[64,2048]{1,0:T(8,128)(2,1)S(1)} %get-tuple-element.73), channel_id=1, source_target_pairs={{0,16},{4,20},{8,24},{12,28},{16,0},{20,4},{24,8},{28,12},{1,17},{... | collective-permute-start | bytes 786440 | tf_op jit(solution)/shard_map/ppermute | solution.py:597
  44.4 11.3 %collective-permute-start.4 = (bf16[64,2048]{1,0:T(8,128)(2,1)S(1)}, bf16[64,2048]{1,0:T(8,128)(2,1)S(1)}, u32[]{:S(2)}, u32[]{:S(2)}) collective-permute-start(bf16[64,2048]{1,0:T(8,128)(2,1)S(1)} %get-tuple-element.74), channel_id=1, source_target_pairs={{0,24},{4,28},{8,16},{12,20},{16,8},{20,12},{24,0},{28,4},{1,25},{... | collective-permute-start | bytes 786440 | tf_op jit(solution)/shard_map/ppermute | solution.py:597
  45.9 13.2 %collective-permute-start.16 = (bf16[1024,256]{1,0:T(8,128)(2,1)S(1)}, bf16[1024,256]{1,0:T(8,128)(2,1)S(1)}, u32[]{:S(2)}, u32[]{:S(2)}) collective-permute-start(bf16[1024,256]{1,0:T(8,128)(2,1)S(1)} %collective-permute-done.6.refs_6_.refs_4_), channel_id=1, source_target_pairs={{1,0},{2,3},{5,4},{6,7},{9,8},{10,11},{13,12},{14,15},{17,16},{18,... | collective-permute-start | bytes 1572872 | tf_op jit(solution)/shard_map/ppermute | solution.py:591
  52.0 7.2 %collective-permute-start.7 = (bf16[1024,256]{1,0:T(8,128)(2,1)S(1)}, bf16[1024,256]{1,0:T(8,128)(2,1)S(1)}, u32[]{:S(2)}, u32[]{:S(2)}) collective-permute-start(bf16[1024,256]{1,0:T(8,128)(2,1)S(1)} %copy-done.1), channel_id=1, source_target_pairs={{0,4},{4,0},{8,12},{12,8},{16,20},{20,16},{24,28},{28,24},{1,5},{5... | collective-permute-start | bytes 1572872 | tf_op jit(solution)/shard_map/ppermute | solution.py:594
  55.7 3.9 %collective-permute-start.9 = (bf16[1024,256]{1,0:T(8,128)(2,1)S(1)}, bf16[1024,256]{1,0:T(8,128)(2,1)S(1)}, u32[]{:S(2)}, u32[]{:S(2)}) collective-permute-start(bf16[1024,256]{1,0:T(8,128)(2,1)S(1)} %collective-permute-done.6.refs_6_.refs_4_), channel_id=1, source_target_pairs={{0,4},{4,0},{8,12},{12,8},{16,20},{20,16},{24,28},{28,24},{1,5},{5... | collective-permute-start | bytes 1572872 | tf_op jit(solution)/shard_map/ppermute | solution.py:594
  56.9 6.9 %collective-permute-start.17 = (bf16[1024,256]{1,0:T(8,128)(2,1)S(1)}, bf16[1024,256]{1,0:T(8,128)(2,1)S(1)}, u32[]{:S(2)}, u32[]{:S(2)}) collective-permute-start(bf16[1024,256]{1,0:T(8,128)(2,1)S(1)} %collective-permute-done.15.refs_4_.refs_2_), channel_id=1, source_target_pairs={{0,4},{4,0},{8,12},{12,8},{16,20},{20,16},{24,28},{28,24},{1,5},{5... | collective-permute-start | bytes 1572872 | tf_op jit(solution)/shard_map/ppermute | solution.py:594
  59.1 5.1 %collective-permute-start.18 = (bf16[1024,256]{1,0:T(8,128)(2,1)S(1)}, bf16[1024,256]{1,0:T(8,128)(2,1)S(1)}, u32[]{:S(2)}, u32[]{:S(2)}) collective-permute-start(bf16[1024,256]{1,0:T(8,128)(2,1)S(1)} %collective-permute-done.16.refs_5_.refs_3_), channel_id=1, source_target_pairs={{0,4},{4,0},{8,12},{12,8},{16,20},{20,16},{24,28},{28,24},{1,5},{5... | collective-permute-start | bytes 1572872 | tf_op jit(solution)/shard_map/ppermute | solution.py:594
  59.1 17.3 %collective-permute-start.30 = (bf16[64,1024]{1,0:T(8,128)(2,1)S(1)}, bf16[64,1024]{1,0:T(8,128)(2,1)S(1)}, u32[]{:S(2)}, u32[]{:S(2)}) collective-permute-start(bf16[64,1024]{1,0:T(8,128)(2,1)S(1)} %shard_map.131.first_ref), channel_id=1, source_target_pairs={{0,8},{4,12},{8,0},{12,4},{16,24},{20,28},{24,16},{28,20},{1,9},{5... | collective-permute-start | bytes 393224 | tf_op jit(solution)/shard_map/ppermute | solution.py:597
  60.7 9.0 %collective-permute-start.10 = (bf16[64,768]{1,0:T(8,128)(2,1)S(1)}, bf16[64,768]{1,0:T(8,128)(2,1)S(1)}, u32[]{:S(2)}, u32[]{:S(2)}) collective-permute-start(bf16[64,768]{1,0:T(8,128)(2,1)S(1)} %get-tuple-element.76), channel_id=1, source_target_pairs={{0,8},{4,12},{8,0},{12,4},{16,24},{20,28},{24,16},{28,20},{1,9},{5... | collective-permute-start | bytes 294920 | tf_op jit(solution)/shard_map/ppermute | solution.py:597
  62.3 8.9 %collective-permute-start.11 = (bf16[64,768]{1,0:T(8,128)(2,1)S(1)}, bf16[64,768]{1,0:T(8,128)(2,1)S(1)}, u32[]{:S(2)}, u32[]{:S(2)}) collective-permute-start(bf16[64,768]{1,0:T(8,128)(2,1)S(1)} %get-tuple-element.77), channel_id=1, source_target_pairs={{0,16},{4,20},{8,24},{12,28},{16,0},{20,4},{24,8},{28,12},{1,17},{... | collective-permute-start | bytes 294920 | tf_op jit(solution)/shard_map/ppermute | solution.py:597
  63.8 7.4 %collective-permute-start.12 = (bf16[64,768]{1,0:T(8,128)(2,1)S(1)}, bf16[64,768]{1,0:T(8,128)(2,1)S(1)}, u32[]{:S(2)}, u32[]{:S(2)}) collective-permute-start(bf16[64,768]{1,0:T(8,128)(2,1)S(1)} %get-tuple-element.78), channel_id=1, source_target_pairs={{0,24},{4,28},{8,16},{12,20},{16,8},{20,12},{24,0},{28,4},{1,25},{... | collective-permute-start | bytes 294920 | tf_op jit(solution)/shard_map/ppermute | solution.py:597
  64.9 6.5 %collective-permute-start.19 = (bf16[64,256]{1,0:T(8,128)(2,1)S(1)}, bf16[64,256]{1,0:T(8,128)(2,1)S(1)}, u32[]{:S(2)}, u32[]{:S(2)}) collective-permute-start(bf16[64,256]{1,0:T(8,128)(2,1)S(1)} %get-tuple-element.83), channel_id=1, source_target_pairs={{0,8},{4,12},{8,0},{12,4},{16,24},{20,28},{24,16},{28,20},{1,9},{5... | collective-permute-start | bytes 98312 | tf_op jit(solution)/shard_map/ppermute | solution.py:597
  71.2 4.8 %collective-permute-start.21 = (bf16[64,256]{1,0:T(8,128)(2,1)S(1)}, bf16[64,256]{1,0:T(8,128)(2,1)S(1)}, u32[]{:S(2)}, u32[]{:S(2)}) collective-permute-start(bf16[64,256]{1,0:T(8,128)(2,1)S(1)} %get-tuple-element.85), channel_id=1, source_target_pairs={{0,24},{4,28},{8,16},{12,20},{16,8},{20,12},{24,0},{28,4},{1,25},{... | collective-permute-start | bytes 98312 | tf_op jit(solution)/shard_map/ppermute | solution.py:597
  71.2 5.8 %collective-permute-start.13 = (bf16[64,256]{1,0:T(8,128)(2,1)S(1)}, bf16[64,256]{1,0:T(8,128)(2,1)S(1)}, u32[]{:S(2)}, u32[]{:S(2)}) collective-permute-start(bf16[64,256]{1,0:T(8,128)(2,1)S(1)} %get-tuple-element.80), channel_id=1, source_target_pairs={{0,1},{1,0},{2,3},{3,2},{4,5},{5,4},{6,7},{7,6},{8,9},{9,8},{10,11... | collective-permute-start | bytes 98312 | tf_op jit(solution)/shard_map/ppermute | solution.py:591
  71.3 5.7 %collective-permute-start.14 = (bf16[64,256]{1,0:T(8,128)(2,1)S(1)}, bf16[64,256]{1,0:T(8,128)(2,1)S(1)}, u32[]{:S(2)}, u32[]{:S(2)}) collective-permute-start(bf16[64,256]{1,0:T(8,128)(2,1)S(1)} %get-tuple-element.81), channel_id=1, source_target_pairs={{0,2},{1,3},{2,0},{3,1},{4,6},{5,7},{6,4},{7,5},{8,10},{9,11},{10,... | collective-permute-start | bytes 98312 | tf_op jit(solution)/shard_map/ppermute | solution.py:591
  76.0 5.8 %collective-permute-start.22 = (bf16[64,256]{1,0:T(8,128)(2,1)S(1)}, bf16[64,256]{1,0:T(8,128)(2,1)S(1)}, u32[]{:S(2)}, u32[]{:S(2)}) collective-permute-start(bf16[64,256]{1,0:T(8,128)(2,1)S(1)} %shard_map.128), channel_id=1, source_target_pairs={{0,3},{1,2},{2,1},{3,0},{4,7},{5,6},{6,5},{7,4},{8,11},{9,10},{10,... | collective-permute-start | bytes 98312 | tf_op jit(solution)/shard_map/ppermute | solution.py:591
  76.5 7.0 %collective-permute-start.31 = (bf16[128,1024]{1,0:T(8,128)(2,1)S(1)}, bf16[128,1024]{1,0:T(8,128)(2,1)S(1)}, u32[]{:S(2)}, u32[]{:S(2)}) collective-permute-start(bf16[128,1024]{1,0:T(8,128)(2,1)S(1)} %shard_map.132.refs_0_), channel_id=1, source_target_pairs={{0,16},{4,20},{8,24},{12,28},{16,0},{20,4},{24,8},{28,12},{1,17},{... | collective-permute-start | bytes 786440 | tf_op jit(solution)/shard_map/ppermute | solution.py:597
  84.7 6.5 %collective-permute-start.26 = (f32[8,128]{1,0:T(8,128)S(1)}, f32[8,128]{1,0:T(8,128)S(1)}, u32[]{:S(2)}, u32[]{:S(2)}) collective-permute-start(f32[8,128]{1,0:T(8,128)S(1)} %shard_map.130.refs_0_), channel_id=1, source_target_pairs={{0,24},{4,28},{8,16},{12,20},{16,8},{20,12},{24,0},{28,4},{1,25},{... | collective-permute-start | bytes 12296 | tf_op jit(solution)/shard_map/ppermute | solution.py:597
  87.1 14.2 %collective-permute-start.32 = (bf16[64,2048]{1,0:T(8,128)(2,1)S(1)}, bf16[64,2048]{1,0:T(8,128)(2,1)S(1)}, u32[]{:S(2)}, u32[]{:S(2)}) collective-permute-start(bf16[64,2048]{1,0:T(8,128)(2,1)S(1)} %get-tuple-element.92), channel_id=1, source_target_pairs={{0,8},{4,12},{8,0},{12,4},{16,24},{20,28},{24,16},{28,20},{1,9},{5... | collective-permute-start | bytes 786440 | tf_op jit(solution)/shard_map/ppermute | solution.py:597
  87.5 13.8 %collective-permute-start.33 = (bf16[64,2048]{1,0:T(8,128)(2,1)S(1)}, bf16[64,2048]{1,0:T(8,128)(2,1)S(1)}, u32[]{:S(2)}, u32[]{:S(2)}) collective-permute-start(bf16[64,2048]{1,0:T(8,128)(2,1)S(1)} %get-tuple-element.93), channel_id=1, source_target_pairs={{0,16},{4,20},{8,24},{12,28},{16,0},{20,4},{24,8},{28,12},{1,17},{... | collective-permute-start | bytes 786440 | tf_op jit(solution)/shard_map/ppermute | solution.py:597
  89.1 12.3 %collective-permute-start.34 = (bf16[64,2048]{1,0:T(8,128)(2,1)S(1)}, bf16[64,2048]{1,0:T(8,128)(2,1)S(1)}, u32[]{:S(2)}, u32[]{:S(2)}) collective-permute-start(bf16[64,2048]{1,0:T(8,128)(2,1)S(1)} %get-tuple-element.94), channel_id=1, source_target_pairs={{0,24},{4,28},{8,16},{12,20},{16,8},{20,12},{24,0},{28,4},{1,25},{... | collective-permute-start | bytes 786440 | tf_op jit(solution)/shard_map/ppermute | solution.py:597
  90.7 10.6 %collective-permute-start.25 = (f32[8,128]{1,0:T(8,128)S(1)}, f32[8,128]{1,0:T(8,128)S(1)}, u32[]{:S(2)}, u32[]{:S(2)}) collective-permute-start(f32[8,128]{1,0:T(8,128)S(1)} %shard_map.130.refs_0_), channel_id=1, source_target_pairs={{0,16},{4,20},{8,24},{12,28},{16,0},{20,4},{24,8},{28,12},{1,17},{... | collective-permute-start | bytes 12296 | tf_op jit(solution)/shard_map/ppermute | solution.py:597
  91.2 10.1 %collective-permute-start.24 = (f32[8,128]{1,0:T(8,128)S(1)}, f32[8,128]{1,0:T(8,128)S(1)}, u32[]{:S(2)}, u32[]{:S(2)}) collective-permute-start(f32[8,128]{1,0:T(8,128)S(1)} %shard_map.130.refs_0_), channel_id=1, source_target_pairs={{0,8},{4,12},{8,0},{12,4},{16,24},{20,28},{24,16},{28,20},{1,9},{5... | collective-permute-start | bytes 12296 | tf_op jit(solution)/shard_map/ppermute | solution.py:597
  (10 other events, 82.1 us)
